TPU v7x, 32 devices: a whole 2x2x4 slice. The times are simulated.
32 devices in a mesh: rows: 16 (over z, y, x), cols: 2 (over core).
Axes of the slice: x: 2, y: 2, z: 4, core: 2. Of those that a mesh axis runs over, the one named last changes fastest.
Arguments:
- eigvecs: float32 [4096, 2048], P('rows', 'cols'), may hold values from -6 to 6
- reflectors: float32 [32, 4096], P('cols', 'rows'), may hold values from -17 to 17
- starts: int32 [32], replicated, may hold values from 0 to 63
Outputs:
- rotated: float32 [4096, 2048], P('rows', 'cols')
Inputs may be any that keep to these rules, and one draw needn't show every extreme that they name: Sweep j's windows begin at rows starts[j] + k * 64.
All inputs are finite; a program needn't handle non-finite values.
Results may differ from a plain program's by a relative error of at most 0.00011.
Values sent between devices are 32-bit elements; how exact they have to be, the bound alone decides.
A program may use at most 64 MiB of HBM per device.

v0:
```python
import functools
import jax
import jax.numpy as jnp
from jax import lax
from jax.experimental import pallas as pl
from jax.experimental.pallas import tpu as pltpu
from jax.sharding import PartitionSpec as P

BAND = 64
MESH = pl.DeviceIdType.MESH
HIGH = lax.Precision.HIGHEST


def dot(a, b, ca=1, cb=0):
    return lax.dot_general(
        a, b, (((ca,), (cb,)), ((), ())), precision=HIGH, preferred_element_type=jnp.float32
    )


def halves(a):
    high = a.astype(jnp.bfloat16)
    return high, (a - high.astype(jnp.float32)).astype(jnp.bfloat16)


def dot_split(a, b, ca=1, cb=0):
    def one(left, right):
        return lax.dot_general(
            left, right, (((ca,), (cb,)), ((), ())), preferred_element_type=jnp.float32)
    return one(a[0], b[0]) + (one(a[0], b[1]) + one(a[1], b[0]))


def sweep_ids(shape, axis, sweeps):
    return lax.broadcasted_iota(jnp.int32, shape, axis) % sweeps


def lower(gram, sweeps):
    return jnp.where(sweep_ids(gram.shape, 0, sweeps) > sweep_ids(gram.shape, 1, sweeps), gram, 0.0)


def on_diagonal(shape):
    return lax.broadcasted_iota(jnp.int32, shape, 0) == lax.broadcasted_iota(jnp.int32, shape, 1)


def inverse(full, sweeps, span):
    eye = on_diagonal(full.shape)
    diag = jnp.where(eye, full, 0.0)
    down = jnp.sum(diag, axis=1, keepdims=True)
    across = jnp.sum(diag, axis=0, keepdims=True)
    down = 1.0 / jnp.where(down == 0.0, 1.0, down)
    across = 1.0 / jnp.where(across == 0.0, 1.0, across)
    rows = sweep_ids(full.shape, 0, sweeps)
    cols = sweep_ids(full.shape, 1, sweeps)
    done = jnp.where(eye, down, 0.0)
    size = 1
    while size < span:
        part = (rows // (2 * size) == cols // (2 * size)) & (rows // size > cols // size)
        off = jnp.where(part, full, 0.0)
        if size == 1:
            done = done - down * off * across
        else:
            done = done - dot(done, dot(off, done))
        size *= 2
    return done


def kernel(nrows, ncols, x_hbm, v_hbm, starts_hbm, ax_hbm, cm_hbm, y_hbm, x_ref, v_all, starts_ref,
           lt_ref, lt_in, q_own, q_send, q_near, q_far, p_ref, x_sem, s_sem, v_local, v_send, v_recv,
           l_send, l_recv, q_send_sem, q_recv_sem, ax_ref, cm_ref, y_ref, out_sem, y_sem):
    d, c = lax.axis_index("rows"), lax.axis_index("cols")
    own = v_hbm.shape[0]
    sweeps = v_all.shape[0]
    height, width = x_ref.shape
    depth = height // BAND
    group = 2 * depth
    rounds = sweeps // group
    place = v_all.at[pl.ds(pl.multiple_of(c * own, own), own)]
    mine = pltpu.make_async_copy(v_hbm, place, v_local)
    mine.start()
    begins = pltpu.make_async_copy(starts_hbm, starts_ref, s_sem)
    begins.start()
    load = pltpu.make_async_copy(x_hbm, x_ref, x_sem)
    load.start()

    offsets = (-2, -1, 1, 2)

    def there(offset):
        return d + offset >= 0 if offset < 0 else d + offset < nrows

    barrier = pltpu.get_barrier_semaphore()
    for offset in offsets:
        @pl.when(there(offset))
        def _():
            pl.semaphore_signal(barrier, inc=1, device_id=(d + offset, c), device_id_type=MESH)
    for step in range(1, ncols):
        pl.semaphore_signal(barrier, inc=1, device_id=(d, (c + step) % ncols), device_id_type=MESH)
    for i, offset in enumerate(offsets):
        @pl.when(jnp.logical_not(there(offset)))
        def _():
            lt_in[i] = jnp.zeros_like(lt_in[i])
            if abs(offset) == 1:
                q_near[i - 1] = jnp.zeros_like(q_near[0])
            else:
                q_far[i // 3] = jnp.zeros_like(q_far[0])
    y_ref[...] = jnp.zeros_like(y_ref)
    peers = sum(there(offset).astype(jnp.int32) for offset in offsets)
    pl.semaphore_wait(barrier, peers + (ncols - 1))

    mine.wait()
    copies = []
    for step in range(1, ncols):
        copy = pltpu.make_async_remote_copy(
            src_ref=place, dst_ref=place, send_sem=v_send.at[step - 1], recv_sem=v_recv.at[step - 1],
            device_id=(d, (c + step) % ncols), device_id_type=MESH)
        copy.start()
        copies.append(copy)
    begins.wait()
    across = jnp.broadcast_to(starts_ref[...], (sweeps, sweeps))
    begin = jnp.sum(jnp.where(on_diagonal(across.shape), across, 0), axis=1, keepdims=True)
    for copy in copies:
        copy.wait()
    v = v_all[...]
    row = lax.broadcasted_iota(jnp.int32, v.shape, 1)
    window = (row - begin + BAND) // BAND
    outside = ((window == 0) & (d == 0)) | ((window == depth) & (d == nrows - 1) & (begin > 0))
    v = jnp.where(outside, 0.0, v)
    parts = [jnp.where(window == k, v, 0.0) for k in range(depth + 1)]
    u_s = jnp.concatenate([parts[0], parts[depth]], axis=0)
    u_i = jnp.concatenate(parts[1:depth], axis=0)
    half_s = 0.5 * jnp.sum(u_s * u_s, axis=1, keepdims=True)
    half_i = 0.5 * jnp.sum(u_i * u_i, axis=1, keepdims=True)
    g_ii = dot(u_i, u_i, 1, 1)
    n_si = lower(dot(u_s, u_i, 1, 1), sweeps)
    n_is = lower(dot(u_i, u_s, 1, 1), sweeps)
    g_ss = dot(u_s, u_s, 1, 1)
    l_ii = jnp.where(on_diagonal(g_ii.shape), half_i, lower(g_ii, sweeps))
    n_ss = jnp.where(on_diagonal(g_ss.shape), half_s, lower(g_ss, sweeps))
    t = inverse(l_ii, sweeps, sweeps)
    f = dot(t, n_is)
    lt = n_ss - dot(n_si, f)
    lt_ref[...] = lt

    def exchange(i, offset, src, dst, send, recv):
        return pltpu.make_async_remote_copy(
            src_ref=src, dst_ref=dst, send_sem=send, recv_sem=recv,
            device_id=(d + offset, c), device_id_type=MESH)

    def lt_copy(i, offset, slot):
        return exchange(i, offset, lt_ref, lt_in.at[slot], l_send.at[i], l_recv.at[slot])

    def q_copy(i, offset, r, slot):
        side = 0 if offset < 0 else 1
        if abs(offset) == 1:
            src, dst = q_send.at[side, r], q_near.at[slot - 1, r]
        else:
            src, dst = q_send.at[side, r, 0], q_far.at[slot // 3, r]
        return exchange(i, offset, src, dst, q_send_sem.at[i, r], q_recv_sem.at[slot, r])

    for i, offset in enumerate(offsets):
        @pl.when(there(offset))
        def _():
            lt_copy(i, offset, 3 - i).start()

    e = dot(t, u_i)
    b = u_s - dot(n_si, e)
    load.wait()
    x_halves = halves(x_ref[...])
    p_ref[...] = dot_split(halves(b), x_halves)

    def near_rows(ref, r):
        return jnp.concatenate(
            [ref[pl.ds(group * r, group)], ref[pl.ds(sweeps + group * r, group)]], axis=0)

    def send_round(r):
        q = near_rows(p_ref, r)
        if r > 0:
            q = q - dot_split(halves(near_rows(lt_ref, r)), halves(y_ref[...]))
        q_own[r] = q
        for side in range(2):
            for part in range(2):
                q_send[side, r, part] = q[side * group + part * depth:side * group + (part + 1) * depth]
            q_send[side, r, 2] = q[(1 - side) * group:(1 - side) * group + depth]
        for i, offset in enumerate(offsets):
            @pl.when(there(offset))
            def _():
                q_copy(i, offset, r, 3 - i).start()

    send_round(0)
    u_t = u_i.T
    cm_ref[...] = u_s.T - dot(u_t, f)
    inner = dot_split(halves(e), x_halves)
    ax_ref[...] = x_ref[...] - dot_split(halves(u_t), halves(inner))
    outs = [pltpu.make_async_copy(ax_ref, ax_hbm, out_sem.at[0]),
            pltpu.make_async_copy(cm_ref, cm_hbm, out_sem.at[1])]
    for out in outs:
        out.start()

    for i, offset in enumerate(offsets):
        @pl.when(there(offset))
        def _():
            lt_copy(i, offset, i).wait_recv()
            lt_copy(i, offset, 3 - i).wait_send()

    def placed(block, at):
        size, total = block.shape[0], 4 * sweeps
        up = (lax.broadcasted_iota(jnp.int32, (total, size), 0)
              == lax.broadcasted_iota(jnp.int32, (total, size), 1) + at)
        up = up.astype(jnp.float32)
        return dot(dot(up, block), up, 1, 1)

    shape = lt.shape
    r_of = lax.broadcasted_iota(jnp.int32, shape, 0) // sweeps
    c_of = lax.broadcasted_iota(jnp.int32, shape, 1) // sweeps
    big = placed(lt_in[1], 0) + placed(lt, sweeps) + placed(lt_in[2], 2 * sweeps)
    big = big + placed(jnp.where((r_of == 1) & (c_of == 1), lt_in[0], 0.0), -sweeps)
    big = big + placed(jnp.where((r_of == 0) & (c_of == 0), lt_in[3], 0.0), 3 * sweeps)
    s = inverse(big, sweeps, group)

    compact = []
    for r in range(rounds):
        at = group * r
        pick = jnp.concatenate(
            [s[sweeps + at:sweeps + at + group], s[2 * sweeps + at:2 * sweeps + at + group]], axis=0)
        from_col = lax.broadcasted_iota(jnp.int32, (4 * sweeps, 4 * group), 0)
        to_col = lax.broadcasted_iota(jnp.int32, (4 * sweeps, 4 * group), 1)
        same = from_col == to_col // group * sweeps + at + to_col % group
        compact.append(halves(dot(pick, same.astype(jnp.float32))))

    for r in range(rounds):
        for i, offset in enumerate(offsets):
            @pl.when(there(offset))
            def _():
                q_copy(i, offset, r, i).wait_recv()
        at = group * r
        zero = jnp.zeros((depth, width), jnp.float32)
        rhs = jnp.concatenate([
            q_far[0, r] + q_near[0, r, 2],
            zero,
            q_near[0, r, 0] + q_own[r, pl.ds(0, depth)],
            q_near[0, r, 1] + q_own[r, pl.ds(depth, depth)],
            q_near[1, r, 0] + q_own[r, pl.ds(group, depth)],
            q_near[1, r, 1] + q_own[r, pl.ds(group + depth, depth)],
            q_near[1, r, 2] + q_far[1, r],
            zero,
        ], axis=0)
        y = dot_split(compact[r], halves(rhs))
        y_ref[pl.ds(at, group)] = y[:group]
        y_ref[pl.ds(sweeps + at, group)] = y[group:]
        if r + 1 < rounds:
            send_round(r + 1)
        for side in range(2):
            rows = pl.ds(side * sweeps + at, group)
            outs.append(pltpu.make_async_copy(y_ref.at[rows], y_hbm.at[rows], y_sem.at[side, r]))
            outs[-1].start()

    for r in range(rounds):
        for i, offset in enumerate(offsets):
            @pl.when(there(offset))
            def _():
                q_copy(i, offset, r, 3 - i).wait_send()
    for out in outs:
        out.wait()


def finish(ax_ref, cm_ref, y_ref, out_ref):
    out_ref[...] = ax_ref[...] - dot_split(halves(cm_ref[...]), halves(y_ref[...]))


def per_device(nrows, ncols, eigvecs, reflectors, starts):
    own, height = reflectors.shape
    width = eigvecs.shape[1]
    sweeps = starts.shape[0]
    group = 2 * (height // BAND)
    rounds = sweeps // group
    f32 = jnp.float32
    hbm = pl.BlockSpec(memory_space=pl.ANY)
    ax, cm, y = pl.pallas_call(
        functools.partial(kernel, nrows, ncols),
        out_shape=(jax.ShapeDtypeStruct((height, width), f32),
                   jax.ShapeDtypeStruct((height, 2 * sweeps), f32),
                   jax.ShapeDtypeStruct((2 * sweeps, width), f32)),
        in_specs=[hbm, hbm, hbm],
        out_specs=(hbm, hbm, hbm),
        scratch_shapes=[
            pltpu.VMEM((height, width), f32),
            pltpu.VMEM((sweeps, height), f32),
            pltpu.VMEM((1, sweeps), jnp.int32),
            pltpu.VMEM((2 * sweeps, 2 * sweeps), f32),
            pltpu.VMEM((4, 2 * sweeps, 2 * sweeps), f32),
            pltpu.VMEM((rounds, 2 * group, width), f32),
            pltpu.VMEM((2, rounds, 3, group // 2, width), f32),
            pltpu.VMEM((2, rounds, 3, group // 2, width), f32),
            pltpu.VMEM((2, rounds, group // 2, width), f32),
            pltpu.VMEM((2 * sweeps, width), f32),
            pltpu.SemaphoreType.DMA,
            pltpu.SemaphoreType.DMA,
            pltpu.SemaphoreType.DMA,
            pltpu.SemaphoreType.DMA((ncols - 1,)),
            pltpu.SemaphoreType.DMA((ncols - 1,)),
            pltpu.SemaphoreType.DMA((4,)),
            pltpu.SemaphoreType.DMA((4,)),
            pltpu.SemaphoreType.DMA((4, rounds)),
            pltpu.SemaphoreType.DMA((4, rounds)),
            pltpu.VMEM((height, width), f32),
            pltpu.VMEM((height, 2 * sweeps), f32),
            pltpu.VMEM((2 * sweeps, width), f32),
            pltpu.SemaphoreType.DMA((2,)),
            pltpu.SemaphoreType.DMA((2, rounds)),
        ],
        compiler_params=pltpu.CompilerParams(
            collective_id=0, has_side_effects=True),
    )(eigvecs, reflectors, starts.reshape(1, sweeps))
    tile = width // 2
    return pl.pallas_call(
        finish,
        grid=(width // tile,),
        out_shape=jax.ShapeDtypeStruct((height, width), f32),
        in_specs=[pl.BlockSpec((height, tile), lambda i: (0, i)),
                  pl.BlockSpec((height, 2 * sweeps), lambda i: (0, 0)),
                  pl.BlockSpec((2 * sweeps, tile), lambda i: (0, i))],
        out_specs=pl.BlockSpec((height, tile), lambda i: (0, i)),
    )(ax, cm, y)


def solution(mesh):
    in_specs = (P("rows", "cols"), P("cols", "rows"), P())
    out_specs = P("rows", "cols")
    body = functools.partial(per_device, mesh.shape["rows"], mesh.shape["cols"])
    return jax.shard_map(
        body, mesh=mesh, in_specs=in_specs, out_specs=out_specs, check_vma=False
    )
```

profile of v0, /device:TPU:0, one launch (start us, length us, event | category | flops | bytes accessed | tf_op | source)
XLA Modules:
  0.0 30.6 jit_solution(10691092074769122189)
XLA Ops:
  0.0 28.0 %shard_map.37 = (f32[256,1024]{1,0:T(8,128)}, f32[256,64]{1,0:T(8,128)}, f32[64,1024]{1,0:T(8,128)}) custom-call(f32[256,1024]{1,0:T(8,128)} %x_hbm.1, f32[16,256]{1,0:T(8,128)} %v_hbm.1, s32[1,32]{1,0:T(1,128)} %bitcast.1), custom_call_target="tpu_custom_call" | custom-call | tf_op jit(solution)/shard_map/pallas_call | solution.py:276
  28.0 2.6 %shard_map.38 = f32[256,1024]{1,0:T(8,128)} custom-call(f32[256,1024]{1,0:T(8,128)} %get-tuple-element.8.ax_ref, f32[256,64]{1,0:T(8,128)} %get-tuple-element.9.cm_ref, f32[64,1024]{1,0:T(8,128)} %get-tuple-element.10.y_ref), custom_call_target="tpu_custom_call" | custom-call | tf_op jit(solution)/shard_map/pallas_call | solution.py:313
where the time goes:
time: 31.2 us; the launch traced here: 30.6 us
  Pallas kernels  30.6 us (98%)
    pallas_call x1, Pallas kernels, per_device(): pl.pallas_call(functools.partial(kernel, nrows, ncols), out_shape=(jax.Sh...  28 us
    pallas_call x1, Pallas kernels, per_device(): pl.pallas_call(finish, grid=(width // tile,), out_shape=jax.ShapeDtypeStr...  2.63 us

commit v1 on v0

v1 whole, which is shorter than its diff:
```python
import functools
import jax
import jax.numpy as jnp
from jax import lax
from jax.experimental import pallas as pl
from jax.experimental.pallas import tpu as pltpu
from jax.sharding import PartitionSpec as P

BAND = 64
LANES = 128
MESH = pl.DeviceIdType.MESH


def halves(a):
    high = a.astype(jnp.bfloat16)
    return high, (a - high.astype(jnp.float32)).astype(jnp.bfloat16)


def product(a, b, ca=1, cb=0):
    def one(left, right):
        return lax.dot_general(
            left, right, (((ca,), (cb,)), ((), ())), preferred_element_type=jnp.float32)
    return one(a[0], b[0]) + (one(a[0], b[1]) + one(a[1], b[0]))


def dot(a, b, ca=1, cb=0):
    return product(halves(a), halves(b), ca, cb)


def gram(a, b):
    return product(a, b, 1, 1) + lax.dot_general(
        a[1], b[1], (((1,), (1,)), ((), ())), preferred_element_type=jnp.float32)


def lanes_of(a):
    return lax.broadcasted_iota(jnp.int32, a.shape, 1)


def sweep_pair(shape, sweeps):
    rows = lax.broadcasted_iota(jnp.int32, shape, 0) % sweeps
    cols = lax.broadcasted_iota(jnp.int32, shape, 1) % sweeps
    return rows, cols


def lower(full, sweeps):
    rows, cols = sweep_pair(full.shape, sweeps)
    return jnp.where(rows > cols, full, 0.0)


def on_diagonal(shape):
    return lax.broadcasted_iota(jnp.int32, shape, 0) == lax.broadcasted_iota(jnp.int32, shape, 1)


def inverse(full, sweeps):
    eye = on_diagonal(full.shape)
    diag = jnp.where(eye, full, 0.0)
    down = jnp.sum(diag, axis=1, keepdims=True)
    across = jnp.sum(diag, axis=0, keepdims=True)
    down = 1.0 / jnp.where(down == 0.0, 1.0, down)
    across = 1.0 / jnp.where(across == 0.0, 1.0, across)
    rows, cols = sweep_pair(full.shape, sweeps)
    apart = rows ^ cols
    done = jnp.where(eye, down, 0.0)
    done = done - down * jnp.where((apart == 1) & (rows > cols), full, 0.0) * across
    size = 2
    while size < sweeps:
        reach = min(4 * size, sweeps)
        off = jnp.where((apart >= size) & (apart < reach) & (rows > cols), full, 0.0)
        inner = halves(done)
        step = halves(product(inner, halves(off)))
        first = done - product(step, inner)
        if reach > 2 * size:
            twice = product(step, step)
            first = first + dot(twice, first)
        done = first
        size = reach
    return done


def kernel(nrows, ncols, x_hbm, v_hbm, starts_hbm, out_ref, x_ref, v_all, starts_ref, lt_in, p_out,
           p_in, ltp_ref, ltp_in, q_ref, near_in, far_in, y_all, y_in, ax_ref, x_sem, s_sem, v_local,
           v_send, v_recv, l_send, l_recv, p_send, p_recv, b_send, b_recv, q_send, q_recv, y_send, y_recv):
    d, c = lax.axis_index("rows"), lax.axis_index("cols")
    own = v_hbm.shape[0]
    sweeps = v_all.shape[0]
    height, width = x_ref.shape
    depth = height // BAND
    team = p_in.shape[0]
    part = width // team
    half = sweeps // 2
    group, member = d // team, d % team
    groups = nrows // team
    place = v_all.at[pl.ds(pl.multiple_of(c * own, own), own)]
    mine = pltpu.make_async_copy(v_hbm, place, v_local)
    mine.start()
    begins = pltpu.make_async_copy(starts_hbm, starts_ref, s_sem)
    begins.start()
    load = pltpu.make_async_copy(x_hbm, x_ref, x_sem)
    load.start()

    offsets = (-2, -1, 1, 2)

    def there(offset):
        return group + offset >= 0 if offset < 0 else group + offset < groups

    def mate(step):
        return (member + step) % team

    barrier = pltpu.get_barrier_semaphore()
    for step in range(1, ncols):
        pl.semaphore_signal(barrier, inc=1, device_id=(d, (c + step) % ncols), device_id_type=MESH)
    for step in range(1, team):
        pl.semaphore_signal(
            barrier, inc=1, device_id=(group * team + mate(step), c), device_id_type=MESH)
    for offset in offsets:
        @pl.when(there(offset))
        def _():
            pl.semaphore_signal(barrier, inc=1, device_id=(d + offset * team, c), device_id_type=MESH)
    for i, offset in enumerate(offsets):
        @pl.when(jnp.logical_not(there(offset)))
        def _():
            ltp_in[i] = jnp.zeros_like(ltp_in[i])
            if abs(offset) == 1:
                near_in[i - 1] = jnp.zeros_like(near_in[0])
            else:
                far_in[i // 3] = jnp.zeros_like(far_in[0])
    peers = sum(there(offset).astype(jnp.int32) for offset in offsets)
    mine.wait()
    pl.semaphore_wait(barrier, peers + (ncols - 1) + (team - 1))

    copies = []
    for step in range(1, ncols):
        copy = pltpu.make_async_remote_copy(
            src_ref=place, dst_ref=place, send_sem=v_send.at[step - 1], recv_sem=v_recv.at[step - 1],
            device_id=(d, (c + step) % ncols), device_id_type=MESH)
        copy.start()
        copies.append(copy)
    begins.wait()
    across = jnp.broadcast_to(starts_ref[...], (sweeps, sweeps))
    begin = jnp.sum(jnp.where(on_diagonal(across.shape), across, 0), axis=1, keepdims=True)
    load.wait()
    x_halves = halves(x_ref[...])
    for copy in copies:
        copy.wait()

    v = v_all[...]
    row = lax.broadcasted_iota(jnp.int32, v.shape, 1)
    window = (row - begin + BAND) // BAND
    outside = ((window == 0) & (d == 0)) | ((window == depth) & (d == nrows - 1) & (begin > 0))
    v = jnp.where(outside, 0.0, v)
    parts = [jnp.where(window == k, v, 0.0) for k in range(depth + 1)]
    u_s = jnp.concatenate([parts[0], parts[depth]], axis=0)
    u_i = jnp.concatenate(parts[1:depth], axis=0)
    inside = u_i.shape[0]
    edge = 2 * sweeps
    half_s = 0.5 * jnp.sum(u_s * u_s, axis=1, keepdims=True)
    half_i = 0.5 * jnp.sum(u_i * u_i, axis=1, keepdims=True)
    pad = jnp.zeros((LANES - edge, height), jnp.float32)
    us_pad = halves(jnp.concatenate([u_s, pad], axis=0))
    us_h, ui_h = halves(u_s), halves(u_i)
    g_ii = gram(ui_h, ui_h)
    n_is = lower(gram(ui_h, us_pad), sweeps)
    n_si = lower(gram(us_h, ui_h), sweeps)
    g_ss = gram(us_h, us_pad)
    l_ii = jnp.where(on_diagonal(g_ii.shape), half_i, lower(g_ii, sweeps))
    n_ss = jnp.where(on_diagonal(g_ss.shape), half_s, lower(g_ss, sweeps))
    t = inverse(l_ii, sweeps)
    t_h, nis_h = halves(t), halves(n_is)
    k_h = halves(product(halves(n_si), t_h))
    lt_in[member] = n_ss - product(k_h, nis_h)

    def to_mate(step, src, dst, send, recv):
        return pltpu.make_async_remote_copy(
            src_ref=src, dst_ref=dst, send_sem=send.at[step - 1], recv_sem=recv.at[step - 1],
            device_id=(group * team + mate(step), c), device_id_type=MESH)

    def lt_copy(step):
        return to_mate(step, lt_in.at[member], lt_in.at[member], l_send, l_recv)

    def p_copy(step):
        return to_mate(step, p_out.at[mate(step)], p_in.at[member], p_send, p_recv)

    def y_copy(step):
        return to_mate(step, y_all.at[pl.ds(mate(step), 2)], y_in.at[member], y_send, y_recv)

    def to_group(i, src, dst, send, recv, slot):
        return pltpu.make_async_remote_copy(
            src_ref=src, dst_ref=dst, send_sem=send.at[i], recv_sem=recv.at[slot],
            device_id=(d + offsets[i] * team, c), device_id_type=MESH)

    def b_copy(i, slot):
        return to_group(i, ltp_ref, ltp_in.at[slot], b_send, b_recv, slot)

    def q_copy(i, slot):
        if offsets[i] == -2:
            src, dst = q_ref.at[0], far_in.at[1]
        elif offsets[i] == -1:
            src, dst = q_ref.at[pl.ds(0, 3)], near_in.at[1]
        elif offsets[i] == 1:
            src, dst = q_ref.at[pl.ds(2, 3)], near_in.at[0]
        else:
            src, dst = q_ref.at[2], far_in.at[0]
        return to_group(i, src, dst, q_send, q_recv, slot)

    for step in range(1, team):
        lt_copy(step).start()

    w_i = product(ui_h, x_halves)
    wi_h = halves(w_i)
    p = product(us_h, x_halves) - product(k_h, wi_h)
    for j in range(team):
        p_out[j] = p[:, j * part:(j + 1) * part]
    for step in range(1, team):
        p_copy(step).start()
    p_in[member] = p_out[member]

    u_t = u_i.T
    ut_h = halves(u_t)
    inner = product(t_h, wi_h)
    ax_ref[...] = x_ref[...] - product(ut_h, halves(inner))
    f = product(t_h, nis_h)[:, :edge]
    cm_h = halves(u_s.T - product(ut_h, halves(f)))
    cm3 = jnp.concatenate([cm_h[0], cm_h[1], cm_h[0]], axis=1)

    for step in range(1, team):
        lt_copy(step).wait_recv()
    turned = [lt_in[j] if j == 0 else pltpu.roll(lt_in[j], j * sweeps, 1) for j in range(team)]
    blocks = [turned[0][:sweeps]]
    for j in range(1, team):
        blocks.append(turned[j - 1][sweeps:] + turned[j][:sweeps])
    blocks.append(turned[team - 1][sweeps:])
    first = lanes_of(blocks[0]) < sweeps
    keep = [jnp.where(first, 0.0, block) for block in blocks]
    ends = [jnp.where(first, block, 0.0) for block in blocks]
    zero = jnp.zeros((sweeps, LANES), jnp.float32)
    m_ii = jnp.concatenate([zero] + keep[1:team], axis=0)
    m_si = jnp.concatenate([keep[0], keep[team]], axis=0)
    left = [zero] * team
    left[1] = left[1] + ends[1]
    left[team - 1] = left[team - 1] + pltpu.roll(ends[team - 1], sweeps, 1)
    m_is = jnp.concatenate(left, axis=0)
    m_ss = jnp.concatenate([ends[0], pltpu.roll(ends[team], sweeps, 1)], axis=0)
    tt_h = halves(inverse(m_ii, sweeps))
    mis_h = halves(m_is)
    kk_h = halves(product(halves(m_si), tt_h))
    ltp = m_ss - product(kk_h, mis_h)
    ltp_ref[...] = ltp
    for i, offset in enumerate(offsets):
        @pl.when(there(offset))
        def _():
            b_copy(i, 3 - i).start()
    ff_h = halves(product(tt_h, mis_h))

    for step in range(1, team):
        p_copy(step).wait_recv()
    sums = [jnp.zeros((sweeps, part), jnp.float32)]
    for j in range(1, team):
        sums.append(p_in[j - 1, sweeps:] + p_in[j, :sweeps])
    q_i = halves(jnp.concatenate(sums, axis=0))
    q_s = jnp.concatenate([p_in[0, :sweeps], p_in[team - 1, sweeps:]], axis=0)
    q = q_s - product(kk_h, q_i)
    for j in range(4):
        q_ref[j] = q[j * half:(j + 1) * half]
    q_ref[4] = q[:half]
    for i, offset in enumerate(offsets):
        @pl.when(there(offset))
        def _():
            q_copy(i, 3 - i).start()
    z_i = product(tt_h, q_i)

    for i, offset in enumerate(offsets):
        @pl.when(there(offset))
        def _():
            b_copy(i, i).wait_recv()
    far_l = jnp.where((lanes_of(zero) >= sweeps) & (lanes_of(zero) < edge), ltp_in[0, sweeps:], 0.0)
    far_r = jnp.where(first, ltp_in[3, :sweeps], 0.0)
    here = pltpu.roll(ltp_ref[...], sweeps, 1)
    near_l = ltp_in[1]
    near_r = pltpu.roll(ltp_in[2], 2 * sweeps, 1)
    big = jnp.concatenate([
        near_l[:sweeps] + pltpu.roll(far_l, LANES - sweeps, 1),
        near_l[sweeps:] + here[:sweeps],
        here[sweeps:] + near_r[:sweeps],
        near_r[sweeps:] + pltpu.roll(far_r, LANES - sweeps, 1),
    ], axis=0)
    s_h = halves(inverse(big, sweeps)[sweeps:3 * sweeps])

    for i, offset in enumerate(offsets):
        @pl.when(there(offset))
        def _():
            q_copy(i, i).wait_recv()
    none = jnp.zeros((half, part), jnp.float32)
    rhs = jnp.concatenate([
        far_in[0] + near_in[0, 2],
        none,
        near_in[0, 0] + q_ref[0],
        near_in[0, 1] + q_ref[1],
        q_ref[2] + near_in[1, 0],
        q_ref[3] + near_in[1, 1],
        near_in[1, 2] + far_in[1],
        none,
    ], axis=0)
    y_s = product(s_h, halves(rhs))
    y_pad = jnp.concatenate([y_s, jnp.zeros((LANES - edge, part), jnp.float32)], axis=0)
    y_i = z_i - product(ff_h, halves(y_pad))
    y_all[0] = y_s[:sweeps]
    for j in range(1, team):
        y_all[j] = y_i[j * sweeps:(j + 1) * sweeps]
    y_all[team] = y_s[sweeps:]
    for step in range(1, team):
        y_copy(step).start()

    def apply(j, y):
        y_h = halves(y)
        y3 = jnp.concatenate([y_h[0], y_h[0], y_h[1]], axis=0)
        cols = pl.ds(pl.multiple_of(j * part, part), part)
        out_ref[:, cols] = ax_ref[:, cols] - lax.dot_general(
            cm3, y3, (((1,), (0,)), ((), ())), preferred_element_type=jnp.float32)

    apply(member, y_all[pl.ds(member, 2)].reshape(edge, part))
    for step in range(1, team):
        y_copy(step).wait_recv()
        source = mate(team - step)
        apply(source, y_in[source].reshape(edge, part))

    for step in range(1, team):
        lt_copy(step).wait_send()
        p_copy(step).wait_send()
        y_copy(step).wait_send()
    for i, offset in enumerate(offsets):
        @pl.when(there(offset))
        def _():
            b_copy(i, 3 - i).wait_send()
            q_copy(i, 3 - i).wait_send()


def per_device(nrows, ncols, eigvecs, reflectors, starts):
    height, width = eigvecs.shape
    sweeps = starts.shape[0]
    team = sweeps // (2 * (height // BAND))
    part = width // team
    assert team * sweeps == LANES and nrows % team == 0
    f32 = jnp.float32
    hbm = pl.BlockSpec(memory_space=pltpu.HBM)
    dma = pltpu.SemaphoreType.DMA
    return pl.pallas_call(
        functools.partial(kernel, nrows, ncols),
        out_shape=jax.ShapeDtypeStruct((height, width), f32),
        in_specs=[hbm, hbm, hbm],
        out_specs=pl.BlockSpec(memory_space=pltpu.VMEM),
        scratch_shapes=[
            pltpu.VMEM((height, width), f32),
            pltpu.VMEM((sweeps, height), f32),
            pltpu.VMEM((1, sweeps), jnp.int32),
            pltpu.VMEM((team, 2 * sweeps, LANES), f32),
            pltpu.VMEM((team, 2 * sweeps, part), f32),
            pltpu.VMEM((team, 2 * sweeps, part), f32),
            pltpu.VMEM((2 * sweeps, LANES), f32),
            pltpu.VMEM((4, 2 * sweeps, LANES), f32),
            pltpu.VMEM((5, sweeps // 2, part), f32),
            pltpu.VMEM((2, 3, sweeps // 2, part), f32),
            pltpu.VMEM((2, sweeps // 2, part), f32),
            pltpu.VMEM((team + 1, sweeps, part), f32),
            pltpu.VMEM((team, 2, sweeps, part), f32),
            pltpu.VMEM((height, width), f32),
            dma, dma, dma,
            dma((ncols - 1,)), dma((ncols - 1,)),
            dma((team - 1,)), dma((team - 1,)),
            dma((team - 1,)), dma((team - 1,)),
            dma((4,)), dma((4,)),
            dma((4,)), dma((4,)),
            dma((team - 1,)), dma((team - 1,)),
        ],
        compiler_params=pltpu.CompilerParams(
            collective_id=0, has_side_effects=True, vmem_limit_bytes=32 * 1024 * 1024),
    )(*(pltpu.with_memory_space_constraint(a, pltpu.HBM)
        for a in (eigvecs, reflectors, starts.reshape(1, sweeps))))


def solution(mesh):
    in_specs = (P("rows", "cols"), P("cols", "rows"), P())
    out_specs = P("rows", "cols")
    body = functools.partial(per_device, mesh.shape["rows"], mesh.shape["cols"])
    return jax.shard_map(
        body, mesh=mesh, in_specs=in_specs, out_specs=out_specs, check_vma=False
    )
```

time: 31.2 us -> 25.6 us (0.82); the launches traced: 30.6 us -> 25.4 us
  Pallas kernels: 30.6 us -> 24.5 us
  local copies, waits for them, and re-layouts: 0 us -> 0.97 us
    pallas_call x2 -> x1, Pallas kernels: 30.6 us -> 24.5 us  [per_device(): pl.pallas_call(functools.partial(kernel, nrows, ncols), out_shape=jax.Sha...]
    unnamed x0 -> x1, local copies, waits for them, and re-layouts: none -> 0.97 us
where the time goes in v1:
time: 25.6 us; the launch traced here: 25.4 us
  Pallas kernels  24.5 us (96%)
  local copies, waits for them, and re-layouts  0.97 us (4%)
    pallas_call x1, Pallas kernels, per_device(): pl.pallas_call(functools.partial(kernel, nrows, ncols), out_shape=jax.Sha...  24.5 us
    unnamed x1, local copies, waits for them, and re-layouts  0.97 us

profile of v1, /device:TPU:0, one launch (start us, length us, event | category | flops | bytes accessed | tf_op | source)
XLA Modules:
  0.0 25.4 jit_solution(950340317754452563)
XLA Ops:
  0.0 24.5 %shard_map.37 = f32[256,1024]{1,0:T(8,128)S(1)} custom-call(f32[256,1024]{1,0:T(8,128)} %x_hbm.1, f32[16,256]{1,0:T(8,128)} %v_hbm.1, s32[1,32]{1,0:T(1,128)} %bitcast.1), custom_call_target="tpu_custom_call" | custom-call | tf_op jit(solution)/shard_map/pallas_call | solution.py:346
  24.5 1.0 %copy.5 = f32[256,1024]{1,0:T(8,128)} copy(f32[256,1024]{1,0:T(8,128)S(1)} %shard_map.37) | data formatting | bytes 2097152

commit v2 on v1

--- a/solution.py
+++ b/solution.py
@@ -23,13 +23,26 @@
     return one(a[0], b[0]) + (one(a[0], b[1]) + one(a[1], b[0]))
 
 
-def dot(a, b, ca=1, cb=0):
-    return product(halves(a), halves(b), ca, cb)
+def exact(a, b, ca=1, cb=0):
+    return product(a, b, ca, cb) + lax.dot_general(
+        a[1], b[1], (((ca,), (cb,)), ((), ())), preferred_element_type=jnp.float32)
 
 
 def gram(a, b):
-    return product(a, b, 1, 1) + lax.dot_general(
-        a[1], b[1], (((1,), (1,)), ((), ())), preferred_element_type=jnp.float32)
+    return exact(a, b, 1, 1)
+
+
+def packed(a, sweeps):
+    return a[:sweeps] + pltpu.roll(a[sweeps:], 2 * sweeps, 1)
+
+
+def unpacked(a, sweeps):
+    first = lanes_of(a) < 2 * sweeps
+    return jnp.where(first, a, 0.0), jnp.where(first, pltpu.roll(a, 2 * sweeps, 1), 0.0)
+
+
+def turn(a, by):
+    return pltpu.roll(a, by % LANES, 1) if by % LANES else a
 
 
 def lanes_of(a):
@@ -67,19 +80,20 @@
         reach = min(4 * size, sweeps)
         off = jnp.where((apart >= size) & (apart < reach) & (rows > cols), full, 0.0)
         inner = halves(done)
-        step = halves(product(inner, halves(off)))
-        first = done - product(step, inner)
+        step = halves(exact(inner, halves(off)))
+        first = done - exact(step, inner)
         if reach > 2 * size:
-            twice = product(step, step)
-            first = first + dot(twice, first)
+            twice = exact(step, step)
+            first = first + exact(halves(twice), halves(first))
         done = first
         size = reach
     return done
 
 
 def kernel(nrows, ncols, x_hbm, v_hbm, starts_hbm, out_ref, x_ref, v_all, starts_ref, lt_in, p_out,
-           p_in, ltp_ref, ltp_in, q_ref, near_in, far_in, y_all, y_in, ax_ref, x_sem, s_sem, v_local,
-           v_send, v_recv, l_send, l_recv, p_send, p_recv, b_send, b_recv, q_send, q_recv, y_send, y_recv):
+           p_in, ltp_ref, ltp_in, follow, q_ref, near_in, far_in, z_all, z_in, y_in, ax_ref, x_sem, s_sem, v_local,
+           v_send, v_recv, l_send, l_recv, p_send, p_recv, b_send, b_recv, q_send, q_recv, z_send, z_recv,
+           y_send, y_recv, entered, arrived):
     d, c = lax.axis_index("rows"), lax.axis_index("cols")
     own = v_hbm.shape[0]
     sweeps = v_all.shape[0]
@@ -106,16 +120,19 @@
     def mate(step):
         return (member + step) % team
 
+    last = ncols - 1
     barrier = pltpu.get_barrier_semaphore()
-    for step in range(1, ncols):
-        pl.semaphore_signal(barrier, inc=1, device_id=(d, (c + step) % ncols), device_id_type=MESH)
-    for step in range(1, team):
-        pl.semaphore_signal(
-            barrier, inc=1, device_id=(group * team + mate(step), c), device_id_type=MESH)
+    for step in range(team):
+        @pl.when((c != last) | (step > 0))
+        def _():
+            pl.semaphore_signal(
+                barrier, inc=1, device_id=(group * team + mate(step), last), device_id_type=MESH)
     for offset in offsets:
         @pl.when(there(offset))
         def _():
-            pl.semaphore_signal(barrier, inc=1, device_id=(d + offset * team, c), device_id_type=MESH)
+            pl.semaphore_signal(barrier, inc=1, device_id=(d + offset * team, 0), device_id_type=MESH)
+    z_all[0] = jnp.zeros_like(z_all[0])
+    z_all[team] = jnp.zeros_like(z_all[0])
     for i, offset in enumerate(offsets):
         @pl.when(jnp.logical_not(there(offset)))
         def _():
@@ -124,9 +141,17 @@
                 near_in[i - 1] = jnp.zeros_like(near_in[0])
             else:
                 far_in[i // 3] = jnp.zeros_like(far_in[0])
-    peers = sum(there(offset).astype(jnp.int32) for offset in offsets)
     mine.wait()
-    pl.semaphore_wait(barrier, peers + (ncols - 1) + (team - 1))
+
+    @pl.when(c == last)
+    def _():
+        pl.semaphore_wait(barrier, ncols * team - 1)
+        for step in range(1, ncols):
+            pl.semaphore_signal(entered, inc=1, device_id=(d, (c + step) % ncols), device_id_type=MESH)
+
+    @pl.when(c != last)
+    def _():
+        pl.semaphore_wait(entered, 1)
 
     copies = []
     for step in range(1, ncols):
@@ -141,7 +166,7 @@
     load.wait()
     x_halves = halves(x_ref[...])
     for copy in copies:
-        copy.wait()
+        copy.wait_recv()
 
     v = v_all[...]
     row = lax.broadcasted_iota(jnp.int32, v.shape, 1)
@@ -164,10 +189,12 @@
     g_ss = gram(us_h, us_pad)
     l_ii = jnp.where(on_diagonal(g_ii.shape), half_i, lower(g_ii, sweeps))
     n_ss = jnp.where(on_diagonal(g_ss.shape), half_s, lower(g_ss, sweeps))
+    wi_h = halves(product(ui_h, x_halves))
+    w_s = product(us_h, x_halves)
     t = inverse(l_ii, sweeps)
     t_h, nis_h = halves(t), halves(n_is)
-    k_h = halves(product(halves(n_si), t_h))
-    lt_in[member] = n_ss - product(k_h, nis_h)
+    k_h = halves(exact(halves(n_si), t_h))
+    lt_in[member] = packed(n_ss - exact(k_h, nis_h), sweeps)
 
     def to_mate(step, src, dst, send, recv):
         return pltpu.make_async_remote_copy(
@@ -180,8 +207,11 @@
     def p_copy(step):
         return to_mate(step, p_out.at[mate(step)], p_in.at[member], p_send, p_recv)
 
+    def z_copy(step):
+        return to_mate(step, z_all.at[pl.ds(mate(step), 2)], z_in.at[member], z_send, z_recv)
+
     def y_copy(step):
-        return to_mate(step, y_all.at[pl.ds(mate(step), 2)], y_in.at[member], y_send, y_recv)
+        return to_mate(step, y_in.at[member], y_in.at[member], y_send, y_recv)
 
     def to_group(i, src, dst, send, recv, slot):
         return pltpu.make_async_remote_copy(
@@ -205,9 +235,7 @@
     for step in range(1, team):
         lt_copy(step).start()
 
-    w_i = product(ui_h, x_halves)
-    wi_h = halves(w_i)
-    p = product(us_h, x_halves) - product(k_h, wi_h)
+    p = w_s - product(k_h, wi_h)
     for j in range(team):
         p_out[j] = p[:, j * part:(j + 1) * part]
     for step in range(1, team):
@@ -218,21 +246,19 @@
     ut_h = halves(u_t)
     inner = product(t_h, wi_h)
     ax_ref[...] = x_ref[...] - product(ut_h, halves(inner))
-    f = product(t_h, nis_h)[:, :edge]
+    f = exact(t_h, nis_h)[:, :edge]
     cm_h = halves(u_s.T - product(ut_h, halves(f)))
-    cm3 = jnp.concatenate([cm_h[0], cm_h[1], cm_h[0]], axis=1)
 
     for step in range(1, team):
         lt_copy(step).wait_recv()
-    turned = [lt_in[j] if j == 0 else pltpu.roll(lt_in[j], j * sweeps, 1) for j in range(team)]
-    blocks = [turned[0][:sweeps]]
-    for j in range(1, team):
-        blocks.append(turned[j - 1][sweeps:] + turned[j][:sweeps])
-    blocks.append(turned[team - 1][sweeps:])
+    zero = jnp.zeros((sweeps, LANES), jnp.float32)
+    blocks = [zero] * (team + 1)
+    for j in range(team):
+        for side, rows in enumerate(unpacked(lt_in[j], sweeps)):
+            blocks[j + side] = blocks[j + side] + turn(rows, j * sweeps)
     first = lanes_of(blocks[0]) < sweeps
     keep = [jnp.where(first, 0.0, block) for block in blocks]
     ends = [jnp.where(first, block, 0.0) for block in blocks]
-    zero = jnp.zeros((sweeps, LANES), jnp.float32)
     m_ii = jnp.concatenate([zero] + keep[1:team], axis=0)
     m_si = jnp.concatenate([keep[0], keep[team]], axis=0)
     left = [zero] * team
@@ -242,14 +268,33 @@
     m_ss = jnp.concatenate([ends[0], pltpu.roll(ends[team], sweeps, 1)], axis=0)
     tt_h = halves(inverse(m_ii, sweeps))
     mis_h = halves(m_is)
-    kk_h = halves(product(halves(m_si), tt_h))
-    ltp = m_ss - product(kk_h, mis_h)
-    ltp_ref[...] = ltp
+    kk_h = halves(exact(halves(m_si), tt_h))
+    ltp_ref[...] = packed(m_ss - exact(kk_h, mis_h), sweeps)
+    peers = sum(there(offset).astype(jnp.int32) for offset in offsets)
+
+    @pl.when(c == 0)
+    def _():
+        pl.semaphore_wait(barrier, peers * ncols)
+        for step in range(1, ncols):
+            pl.semaphore_signal(arrived, inc=1, device_id=(d, step), device_id_type=MESH)
+
+    @pl.when(c != 0)
+    def _():
+        pl.semaphore_wait(arrived, 1)
+
     for i, offset in enumerate(offsets):
         @pl.when(there(offset))
         def _():
             b_copy(i, 3 - i).start()
-    ff_h = halves(product(tt_h, mis_h))
+    ff = exact(tt_h, mis_h)
+    at_left = jnp.where(on_diagonal(zero.shape), 1.0, 0.0)
+    follow[0] = at_left
+    for j in range(1, team):
+        follow[j] = -ff[j * sweeps:(j + 1) * sweeps]
+    follow[team] = turn(at_left, sweeps)
+    mine_h = halves(follow[pl.ds(member, 2)].reshape(edge, LANES))
+    cf_h = halves(product(cm_h, mine_h)[:, :edge])
+    cf3 = jnp.concatenate([cf_h[0], cf_h[1], cf_h[0]], axis=1)
 
     for step in range(1, team):
         p_copy(step).wait_recv()
@@ -267,21 +312,25 @@
         def _():
             q_copy(i, 3 - i).start()
     z_i = product(tt_h, q_i)
+    for j in range(1, team):
+        z_all[j] = z_i[j * sweeps:(j + 1) * sweeps]
+    for step in range(1, team):
+        z_copy(step).start()
 
     for i, offset in enumerate(offsets):
         @pl.when(there(offset))
         def _():
             b_copy(i, i).wait_recv()
-    far_l = jnp.where((lanes_of(zero) >= sweeps) & (lanes_of(zero) < edge), ltp_in[0, sweeps:], 0.0)
-    far_r = jnp.where(first, ltp_in[3, :sweeps], 0.0)
-    here = pltpu.roll(ltp_ref[...], sweeps, 1)
-    near_l = ltp_in[1]
-    near_r = pltpu.roll(ltp_in[2], 2 * sweeps, 1)
+    here = unpacked(ltp_ref[...], sweeps)
+    near_l = unpacked(ltp_in[1], sweeps)
+    near_r = unpacked(ltp_in[2], sweeps)
+    far_l = unpacked(ltp_in[0], sweeps)[1]
+    far_r = unpacked(ltp_in[3], sweeps)[0]
     big = jnp.concatenate([
-        near_l[:sweeps] + pltpu.roll(far_l, LANES - sweeps, 1),
-        near_l[sweeps:] + here[:sweeps],
-        here[sweeps:] + near_r[:sweeps],
-        near_r[sweeps:] + pltpu.roll(far_r, LANES - sweeps, 1),
+        near_l[0] + turn(jnp.where(first, 0.0, far_l), -sweeps),
+        near_l[1] + turn(here[0], sweeps),
+        turn(here[1], sweeps) + turn(near_r[0], 2 * sweeps),
+        turn(near_r[1], 2 * sweeps) + turn(jnp.where(first, far_r, 0.0), 3 * sweeps),
     ], axis=0)
     s_h = halves(inverse(big, sweeps)[sweeps:3 * sweeps])
 
@@ -301,32 +350,40 @@
         none,
     ], axis=0)
     y_s = product(s_h, halves(rhs))
-    y_pad = jnp.concatenate([y_s, jnp.zeros((LANES - edge, part), jnp.float32)], axis=0)
-    y_i = z_i - product(ff_h, halves(y_pad))
-    y_all[0] = y_s[:sweeps]
-    for j in range(1, team):
-        y_all[j] = y_i[j * sweeps:(j + 1) * sweeps]
-    y_all[team] = y_s[sweeps:]
+    y_in[member] = y_s
     for step in range(1, team):
         y_copy(step).start()
 
-    def apply(j, y):
+    cm3 = jnp.concatenate([cm_h[0], cm_h[1], cm_h[0]], axis=1)
+
+    def apply(left, y):
         y_h = halves(y)
         y3 = jnp.concatenate([y_h[0], y_h[0], y_h[1]], axis=0)
+        return lax.dot_general(left, y3, (((1,), (0,)), ((), ())), preferred_element_type=jnp.float32)
+
+    z_in[member] = z_all[pl.ds(member, 2)]
+    for step in range(1, team):
+        z_copy(step).wait_recv()
+    for j in range(team):
+        cols = slice(j * part, (j + 1) * part)
+        ax_ref[:, cols] = ax_ref[:, cols] - apply(cm3, z_in[j].reshape(edge, part))
+
+    def last_step(j):
         cols = pl.ds(pl.multiple_of(j * part, part), part)
-        out_ref[:, cols] = ax_ref[:, cols] - lax.dot_general(
-            cm3, y3, (((1,), (0,)), ((), ())), preferred_element_type=jnp.float32)
-
-    apply(member, y_all[pl.ds(member, 2)].reshape(edge, part))
+        out_ref[:, cols] = ax_ref[:, cols] - apply(cf3, y_in[j])
+
+    last_step(member)
     for step in range(1, team):
         y_copy(step).wait_recv()
-        source = mate(team - step)
-        apply(source, y_in[source].reshape(edge, part))
-
+        last_step(mate(team - step))
+
+    for copy in copies:
+        copy.wait_send()
     for step in range(1, team):
         lt_copy(step).wait_send()
         p_copy(step).wait_send()
         y_copy(step).wait_send()
+        z_copy(step).wait_send()
     for i, offset in enumerate(offsets):
         @pl.when(there(offset))
         def _():
@@ -352,16 +409,18 @@
             pltpu.VMEM((height, width), f32),
             pltpu.VMEM((sweeps, height), f32),
             pltpu.VMEM((1, sweeps), jnp.int32),
-            pltpu.VMEM((team, 2 * sweeps, LANES), f32),
+            pltpu.VMEM((team, sweeps, LANES), f32),
             pltpu.VMEM((team, 2 * sweeps, part), f32),
             pltpu.VMEM((team, 2 * sweeps, part), f32),
-            pltpu.VMEM((2 * sweeps, LANES), f32),
-            pltpu.VMEM((4, 2 * sweeps, LANES), f32),
+            pltpu.VMEM((sweeps, LANES), f32),
+            pltpu.VMEM((4, sweeps, LANES), f32),
+            pltpu.VMEM((team + 1, sweeps, LANES), f32),
             pltpu.VMEM((5, sweeps // 2, part), f32),
             pltpu.VMEM((2, 3, sweeps // 2, part), f32),
             pltpu.VMEM((2, sweeps // 2, part), f32),
             pltpu.VMEM((team + 1, sweeps, part), f32),
             pltpu.VMEM((team, 2, sweeps, part), f32),
+            pltpu.VMEM((team, 2 * sweeps, part), f32),
             pltpu.VMEM((height, width), f32),
             dma, dma, dma,
             dma((ncols - 1,)), dma((ncols - 1,)),
@@ -370,6 +429,8 @@
             dma((4,)), dma((4,)),
             dma((4,)), dma((4,)),
             dma((team - 1,)), dma((team - 1,)),
+            dma((team - 1,)), dma((team - 1,)),
+            pltpu.SemaphoreType.REGULAR, pltpu.SemaphoreType.REGULAR,
         ],
         compiler_params=pltpu.CompilerParams(
             collective_id=0, has_side_effects=True, vmem_limit_bytes=32 * 1024 * 1024),

time: 25.6 us -> 24.4 us (0.953)
  Pallas kernels: 24.5 us -> 23.3 us
    pallas_call x1, Pallas kernels: 24.5 us -> 23.3 us  [per_device(): pl.pallas_call(functools.partial(kernel, nrows, ncols), out_shape=jax.Sha...]
where the time goes in v2:
time: 24.4 us; the launch traced here: 24.2 us
  Pallas kernels  23.3 us (95%)
  local copies, waits for them, and re-layouts  0.97 us (4%)
    pallas_call x1, Pallas kernels, per_device(): pl.pallas_call(functools.partial(kernel, nrows, ncols), out_shape=jax.Sha...  23.3 us
    unnamed x1, local copies, waits for them, and re-layouts  0.97 us

profile of v2, /device:TPU:0, one launch (start us, length us, event | category | flops | bytes accessed | tf_op | source)
XLA Modules:
  0.0 24.2 jit_solution(17841825036106204070)
XLA Ops:
  0.0 23.3 %shard_map.37 = f32[256,1024]{1,0:T(8,128)S(1)} custom-call(f32[256,1024]{1,0:T(8,128)} %x_hbm.1, f32[16,256]{1,0:T(8,128)} %v_hbm.1, s32[1,32]{1,0:T(1,128)} %bitcast.1), custom_call_target="tpu_custom_call" | custom-call | tf_op jit(solution)/shard_map/pallas_call | solution.py:403
  23.3 1.0 %copy.5 = f32[256,1024]{1,0:T(8,128)} copy(f32[256,1024]{1,0:T(8,128)S(1)} %shard_map.37) | data formatting | bytes 2097152

commit v3 on v2

--- a/solution.py
+++ b/solution.py
@@ -64,7 +64,32 @@
     return lax.broadcasted_iota(jnp.int32, shape, 0) == lax.broadcasted_iota(jnp.int32, shape, 1)
 
 
-def inverse(full, sweeps):
+def seed(full, size):
+    lanes = full.shape[1]
+    eye = on_diagonal(full.shape)
+    diag = jnp.where(eye, full, 0.0)
+    down = jnp.sum(diag, axis=1, keepdims=True)
+    across = jnp.sum(diag, axis=0, keepdims=True)
+    down = 1.0 / jnp.where(down == 0.0, 1.0, down)
+    across = 1.0 / jnp.where(across == 0.0, 1.0, across)
+    rows = lax.broadcasted_iota(jnp.int32, full.shape, 0)
+    cols = lax.broadcasted_iota(jnp.int32, full.shape, 1)
+    scaled = jnp.where((rows ^ cols) < size, down * full, 0.0)
+    below = [jnp.where(rows - cols == m, scaled, 0.0) for m in range(size)]
+    below = [jnp.sum(entries, axis=0, keepdims=True) for entries in below]
+    terms = [across]
+    for k in range(1, size):
+        total = below[k] * across
+        for m in range(1, k):
+            total = total + pltpu.roll(below[m], lanes - (k - m), 1) * terms[k - m]
+        terms.append(-total)
+    done = jnp.where(eye, across, 0.0)
+    for k in range(1, size):
+        done = jnp.where(rows - cols == k, terms[k], done)
+    return done
+
+
+def seed_pairs(full, sweeps):
     eye = on_diagonal(full.shape)
     diag = jnp.where(eye, full, 0.0)
     down = jnp.sum(diag, axis=1, keepdims=True)
@@ -72,28 +97,36 @@
     down = 1.0 / jnp.where(down == 0.0, 1.0, down)
     across = 1.0 / jnp.where(across == 0.0, 1.0, across)
     rows, cols = sweep_pair(full.shape, sweeps)
+    pair = ((rows ^ cols) == 1) & (rows > cols)
+    return jnp.where(eye, down, 0.0) - down * jnp.where(pair, full, 0.0) * across
+
+
+def inverse(full, sweeps, size, done, right=None):
+    rows, cols = sweep_pair(full.shape, sweeps)
     apart = rows ^ cols
-    done = jnp.where(eye, down, 0.0)
-    done = done - down * jnp.where((apart == 1) & (rows > cols), full, 0.0) * across
-    size = 2
     while size < sweeps:
         reach = min(4 * size, sweeps)
         off = jnp.where((apart >= size) & (apart < reach) & (rows > cols), full, 0.0)
         inner = halves(done)
         step = halves(exact(inner, halves(off)))
+        if reach == sweeps and right is not None:
+            done = jnp.concatenate([done, exact(inner, right)], axis=1)
+            inner = halves(done)
         first = done - exact(step, inner)
         if reach > 2 * size:
             twice = exact(step, step)
             first = first + exact(halves(twice), halves(first))
         done = first
         size = reach
-    return done
+    if right is None:
+        return done
+    return done[:, :full.shape[1]], done[:, full.shape[1]:]
 
 
 def kernel(nrows, ncols, x_hbm, v_hbm, starts_hbm, out_ref, x_ref, v_all, starts_ref, lt_in, p_out,
            p_in, ltp_ref, ltp_in, follow, q_ref, near_in, far_in, z_all, z_in, y_in, ax_ref, x_sem, s_sem, v_local,
            v_send, v_recv, l_send, l_recv, p_send, p_recv, b_send, b_recv, q_send, q_recv, z_send, z_recv,
-           y_send, y_recv, entered, arrived):
+           y_send, y_recv, paired, entered, arrived):
     d, c = lax.axis_index("rows"), lax.axis_index("cols")
     own = v_hbm.shape[0]
     sweeps = v_all.shape[0]
@@ -121,16 +154,23 @@
         return (member + step) % team
 
     last = ncols - 1
+    base = group * team
     barrier = pltpu.get_barrier_semaphore()
-    for step in range(team):
-        @pl.when((c != last) | (step > 0))
-        def _():
-            pl.semaphore_signal(
-                barrier, inc=1, device_id=(group * team + mate(step), last), device_id_type=MESH)
+
+    def greet(sem, slab, core):
+        pl.semaphore_signal(sem, inc=1, device_id=(slab, core), device_id_type=MESH)
+
+    @pl.when(c > 0)
+    def _():
+        greet(barrier, d, 0)
+
+    @pl.when((member > 0) | (c < last))
+    def _():
+        greet(barrier, base, last)
     for offset in offsets:
         @pl.when(there(offset))
         def _():
-            pl.semaphore_signal(barrier, inc=1, device_id=(d + offset * team, 0), device_id_type=MESH)
+            greet(barrier, base + offset * team + team - 1, last)
     z_all[0] = jnp.zeros_like(z_all[0])
     z_all[team] = jnp.zeros_like(z_all[0])
     for i, offset in enumerate(offsets):
@@ -143,15 +183,15 @@
                 far_in[i // 3] = jnp.zeros_like(far_in[0])
     mine.wait()
 
-    @pl.when(c == last)
-    def _():
-        pl.semaphore_wait(barrier, ncols * team - 1)
-        for step in range(1, ncols):
-            pl.semaphore_signal(entered, inc=1, device_id=(d, (c + step) % ncols), device_id_type=MESH)
-
-    @pl.when(c != last)
-    def _():
-        pl.semaphore_wait(entered, 1)
+    @pl.when(c == 0)
+    def _():
+        pl.semaphore_wait(barrier, last)
+        for core in range(1, ncols):
+            greet(paired, d, core)
+
+    @pl.when(c > 0)
+    def _():
+        pl.semaphore_wait(paired, 1)
 
     copies = []
     for step in range(1, ncols):
@@ -180,21 +220,25 @@
     edge = 2 * sweeps
     half_s = 0.5 * jnp.sum(u_s * u_s, axis=1, keepdims=True)
     half_i = 0.5 * jnp.sum(u_i * u_i, axis=1, keepdims=True)
+    half_i = jnp.concatenate([half_i, jnp.zeros((LANES - inside, 1), jnp.float32)], axis=0)
     pad = jnp.zeros((LANES - edge, height), jnp.float32)
     us_pad = halves(jnp.concatenate([u_s, pad], axis=0))
+    ui_pad = halves(jnp.concatenate([u_i, jnp.zeros((LANES - inside, height), jnp.float32)], axis=0))
     us_h, ui_h = halves(u_s), halves(u_i)
-    g_ii = gram(ui_h, ui_h)
-    n_is = lower(gram(ui_h, us_pad), sweeps)
-    n_si = lower(gram(us_h, ui_h), sweeps)
+    g_ii = gram(ui_pad, ui_pad)
+    n_is = lower(gram(ui_pad, us_pad), sweeps)
+    n_si = lower(gram(us_h, ui_pad), sweeps)
     g_ss = gram(us_h, us_pad)
     l_ii = jnp.where(on_diagonal(g_ii.shape), half_i, lower(g_ii, sweeps))
     n_ss = jnp.where(on_diagonal(g_ss.shape), half_s, lower(g_ss, sweeps))
     wi_h = halves(product(ui_h, x_halves))
     w_s = product(us_h, x_halves)
-    t = inverse(l_ii, sweeps)
-    t_h, nis_h = halves(t), halves(n_is)
-    k_h = halves(exact(halves(n_si), t_h))
-    lt_in[member] = packed(n_ss - exact(k_h, nis_h), sweeps)
+    t, f = inverse(l_ii, sweeps, 2, seed_pairs(l_ii, sweeps), halves(n_is))
+    nsi_h = halves(n_si)
+    lt_in[member] = packed(n_ss - exact(nsi_h, halves(f)), sweeps)
+    t = t[:, :inside]
+    k_h = halves(exact(nsi_h, halves(t)))
+    t_h = halves(t[:inside])
 
     def to_mate(step, src, dst, send, recv):
         return pltpu.make_async_remote_copy(
@@ -232,6 +276,18 @@
             src, dst = q_ref.at[2], far_in.at[0]
         return to_group(i, src, dst, q_send, q_recv, slot)
 
+    @pl.when((member == 0) & (c == last))
+    def _():
+        pl.semaphore_wait(barrier, ncols * team - 1)
+        for slab in range(team):
+            for core in range(ncols):
+                if slab > 0 or core < last:
+                    greet(entered, base + slab, core)
+
+    @pl.when((member > 0) | (c < last))
+    def _():
+        pl.semaphore_wait(entered, 1)
+
     for step in range(1, team):
         lt_copy(step).start()
 
@@ -241,13 +297,22 @@
     for step in range(1, team):
         p_copy(step).start()
     p_in[member] = p_out[member]
+
+    peers = sum(there(offset).astype(jnp.int32) for offset in offsets)
+
+    @pl.when((member == team - 1) & (c == last))
+    def _():
+        pl.semaphore_wait(barrier, peers * ncols * team)
+        for slab in range(team):
+            for core in range(ncols):
+                if slab < team - 1 or core < last:
+                    greet(arrived, base + slab, core)
 
     u_t = u_i.T
     ut_h = halves(u_t)
     inner = product(t_h, wi_h)
     ax_ref[...] = x_ref[...] - product(ut_h, halves(inner))
-    f = exact(t_h, nis_h)[:, :edge]
-    cm_h = halves(u_s.T - product(ut_h, halves(f)))
+    cm_h = halves(u_s.T - product(ut_h, halves(f[:inside, :edge])))
 
     for step in range(1, team):
         lt_copy(step).wait_recv()
@@ -266,19 +331,10 @@
     left[team - 1] = left[team - 1] + pltpu.roll(ends[team - 1], sweeps, 1)
     m_is = jnp.concatenate(left, axis=0)
     m_ss = jnp.concatenate([ends[0], pltpu.roll(ends[team], sweeps, 1)], axis=0)
-    tt_h = halves(inverse(m_ii, sweeps))
-    mis_h = halves(m_is)
-    kk_h = halves(exact(halves(m_si), tt_h))
-    ltp_ref[...] = packed(m_ss - exact(kk_h, mis_h), sweeps)
-    peers = sum(there(offset).astype(jnp.int32) for offset in offsets)
-
-    @pl.when(c == 0)
-    def _():
-        pl.semaphore_wait(barrier, peers * ncols)
-        for step in range(1, ncols):
-            pl.semaphore_signal(arrived, inc=1, device_id=(d, step), device_id_type=MESH)
-
-    @pl.when(c != 0)
+    tt, ff = inverse(m_ii, sweeps, depth, seed(m_ii, depth), halves(m_is))
+    msi_h = halves(m_si)
+    ltp_ref[...] = packed(m_ss - exact(msi_h, halves(ff)), sweeps)
+    @pl.when((member < team - 1) | (c < last))
     def _():
         pl.semaphore_wait(arrived, 1)
 
@@ -286,16 +342,8 @@
         @pl.when(there(offset))
         def _():
             b_copy(i, 3 - i).start()
-    ff = exact(tt_h, mis_h)
-    at_left = jnp.where(on_diagonal(zero.shape), 1.0, 0.0)
-    follow[0] = at_left
-    for j in range(1, team):
-        follow[j] = -ff[j * sweeps:(j + 1) * sweeps]
-    follow[team] = turn(at_left, sweeps)
-    mine_h = halves(follow[pl.ds(member, 2)].reshape(edge, LANES))
-    cf_h = halves(product(cm_h, mine_h)[:, :edge])
-    cf3 = jnp.concatenate([cf_h[0], cf_h[1], cf_h[0]], axis=1)
-
+    tt_h = halves(tt)
+    kk_h = halves(exact(msi_h, tt_h))
     for step in range(1, team):
         p_copy(step).wait_recv()
     sums = [jnp.zeros((sweeps, part), jnp.float32)]
@@ -317,6 +365,15 @@
     for step in range(1, team):
         z_copy(step).start()
 
+    at_left = jnp.where(on_diagonal(zero.shape), 1.0, 0.0)
+    follow[0] = at_left
+    for j in range(1, team):
+        follow[j] = -ff[j * sweeps:(j + 1) * sweeps]
+    follow[team] = turn(at_left, sweeps)
+    mine_h = halves(follow[pl.ds(member, 2)].reshape(edge, LANES))
+    cf_h = halves(product(cm_h, mine_h)[:, :edge])
+    cf3 = jnp.concatenate([cf_h[0], cf_h[1], cf_h[0]], axis=1)
+
     for i, offset in enumerate(offsets):
         @pl.when(there(offset))
         def _():
@@ -332,7 +389,7 @@
         turn(here[1], sweeps) + turn(near_r[0], 2 * sweeps),
         turn(near_r[1], 2 * sweeps) + turn(jnp.where(first, far_r, 0.0), 3 * sweeps),
     ], axis=0)
-    s_h = halves(inverse(big, sweeps)[sweeps:3 * sweeps])
+    s_h = halves(inverse(big, sweeps, half // 2, seed(big, half // 2))[sweeps:3 * sweeps])
 
     for i, offset in enumerate(offsets):
         @pl.when(there(offset))
@@ -430,7 +487,7 @@
             dma((4,)), dma((4,)),
             dma((team - 1,)), dma((team - 1,)),
             dma((team - 1,)), dma((team - 1,)),
-            pltpu.SemaphoreType.REGULAR, pltpu.SemaphoreType.REGULAR,
+            pltpu.SemaphoreType.REGULAR, pltpu.SemaphoreType.REGULAR, pltpu.SemaphoreType.REGULAR,
         ],
         compiler_params=pltpu.CompilerParams(
             collective_id=0, has_side_effects=True, vmem_limit_bytes=32 * 1024 * 1024),

time: 24.4 us -> 23.5 us (0.963)
  Pallas kernels: 23.3 us -> 22.4 us
    pallas_call x1, Pallas kernels: 23.3 us -> 22.4 us  [per_device(): pl.pallas_call(functools.partial(kernel, nrows, ncols), out_shape=jax.Sha...]
where the time goes in v3:
time: 23.5 us; the launch traced here: 23.4 us
  Pallas kernels  22.4 us (95%)
  local copies, waits for them, and re-layouts  0.97 us (4%)
    pallas_call x1, Pallas kernels, per_device(): pl.pallas_call(functools.partial(kernel, nrows, ncols), out_shape=jax.Sha...  22.4 us
    unnamed x1, local copies, waits for them, and re-layouts  0.97 us

profile of v3, /device:TPU:0, one launch (start us, length us, event | category | flops | bytes accessed | tf_op | source)
XLA Modules:
  0.0 23.4 jit_solution(18375133567717710821)
XLA Ops:
  0.0 22.4 %shard_map.37 = f32[256,1024]{1,0:T(8,128)S(1)} custom-call(f32[256,1024]{1,0:T(8,128)} %x_hbm.1, f32[16,256]{1,0:T(8,128)} %v_hbm.1, s32[1,32]{1,0:T(1,128)} %bitcast.1), custom_call_target="tpu_custom_call" | custom-call | tf_op jit(solution)/shard_map/pallas_call | solution.py:460
  22.4 1.0 %copy.5 = f32[256,1024]{1,0:T(8,128)} copy(f32[256,1024]{1,0:T(8,128)S(1)} %shard_map.37) | data formatting | bytes 2097152

commit v4 on v3

v4 whole, which is shorter than its diff:
```python
import functools
import jax
import jax.numpy as jnp
from jax import lax
from jax.experimental import pallas as pl
from jax.experimental.pallas import tpu as pltpu
from jax.sharding import PartitionSpec as P

BAND = 64
LANES = 128
MESH = pl.DeviceIdType.MESH


def halves(a):
    high = a.astype(jnp.bfloat16)
    return high, (a - high.astype(jnp.float32)).astype(jnp.bfloat16)


def product(a, b, ca=1, cb=0):
    def one(left, right):
        return lax.dot_general(
            left, right, (((ca,), (cb,)), ((), ())), preferred_element_type=jnp.float32)
    return one(a[0], b[0]) + (one(a[0], b[1]) + one(a[1], b[0]))


def exact(a, b):
    left = jnp.concatenate(a, axis=1)
    right = jnp.concatenate(b, axis=1)
    both = lax.dot_general(
        left, jnp.concatenate([right, right], axis=0), (((1,), (0,)), ((), ())),
        preferred_element_type=jnp.float32)
    width = both.shape[1] // 2
    return both[:, :width] + both[:, width:]


def gram(a, b):
    return product(a, b, 1, 1) + lax.dot_general(
        a[1], b[1], (((1,), (1,)), ((), ())), preferred_element_type=jnp.float32)


def packed(a, sweeps):
    return a[:sweeps] + pltpu.roll(a[sweeps:], 2 * sweeps, 1)


def turn(a, by):
    return pltpu.roll(a, by % LANES, 1) if by % LANES else a


def unpacked(a, sweeps, by=0):
    inside = (lanes_of(a) - by) % LANES < 2 * sweeps
    return [jnp.where(inside, turn(a, by + side * 2 * sweeps), 0.0) for side in range(2)]


def lanes_of(a):
    return lax.broadcasted_iota(jnp.int32, a.shape, 1)


def sweep_pair(shape, sweeps):
    rows = lax.broadcasted_iota(jnp.int32, shape, 0) % sweeps
    cols = lax.broadcasted_iota(jnp.int32, shape, 1) % sweeps
    return rows, cols


def lower(full, sweeps):
    rows, cols = sweep_pair(full.shape, sweeps)
    return jnp.where(rows > cols, full, 0.0)


def on_diagonal(shape):
    return lax.broadcasted_iota(jnp.int32, shape, 0) == lax.broadcasted_iota(jnp.int32, shape, 1)


def seed(full, size):
    lanes = full.shape[1]
    eye = on_diagonal(full.shape)
    diag = jnp.where(eye, full, 0.0)
    down = jnp.sum(diag, axis=1, keepdims=True)
    across = jnp.sum(diag, axis=0, keepdims=True)
    down = 1.0 / jnp.where(down == 0.0, 1.0, down)
    across = 1.0 / jnp.where(across == 0.0, 1.0, across)
    rows = lax.broadcasted_iota(jnp.int32, full.shape, 0)
    cols = lax.broadcasted_iota(jnp.int32, full.shape, 1)
    scaled = jnp.where((rows ^ cols) < size, down * full, 0.0)
    below = [jnp.where(rows - cols == m, scaled, 0.0) for m in range(size)]
    below = [jnp.sum(entries, axis=0, keepdims=True) for entries in below]
    terms = [across]
    for k in range(1, size):
        total = below[k] * across
        for m in range(1, k):
            total = total + pltpu.roll(below[m], lanes - (k - m), 1) * terms[k - m]
        terms.append(-total)
    done = jnp.where(eye, across, 0.0)
    for k in range(1, size):
        done = jnp.where(rows - cols == k, terms[k], done)
    return done


def seed_pairs(full, sweeps):
    eye = on_diagonal(full.shape)
    diag = jnp.where(eye, full, 0.0)
    down = jnp.sum(diag, axis=1, keepdims=True)
    across = jnp.sum(diag, axis=0, keepdims=True)
    down = 1.0 / jnp.where(down == 0.0, 1.0, down)
    across = 1.0 / jnp.where(across == 0.0, 1.0, across)
    rows, cols = sweep_pair(full.shape, sweeps)
    pair = ((rows ^ cols) == 1) & (rows > cols)
    return jnp.where(eye, down, 0.0) - down * jnp.where(pair, full, 0.0) * across


def inverse(full, sweeps, size, done, right=None):
    rows, cols = sweep_pair(full.shape, sweeps)
    apart = rows ^ cols
    while size < sweeps:
        reach = min(4 * size, sweeps)
        off = jnp.where((apart >= size) & (apart < reach) & (rows > cols), full, 0.0)
        inner = halves(done)
        step = halves(exact(inner, halves(off)))
        if reach == sweeps and right is not None:
            done = jnp.concatenate([done, exact(inner, right)], axis=1)
            inner = halves(done)
        first = done - exact(step, inner)
        if reach > 2 * size:
            twice = exact(step, step)
            first = first + exact(halves(twice), halves(first))
        done = first
        size = reach
    if right is None:
        return done
    return done[:, :full.shape[1]], done[:, full.shape[1]:]


def kernel(nrows, ncols, x_hbm, v_hbm, starts_hbm, out_ref, x_ref, v_all, starts_ref, lt_in, p_out,
           p_in, ltp_ref, ltp_in, follow, q_ref, near_in, far_in, z_all, z_in, y_in, ax_ref, x_sem, s_sem, v_local,
           v_send, v_recv, l_send, l_recv, p_send, p_recv, b_send, b_recv, q_send, q_recv, z_send, z_recv,
           y_send, y_recv, paired, entered, arrived):
    d, c = lax.axis_index("rows"), lax.axis_index("cols")
    own = v_hbm.shape[0]
    sweeps = v_all.shape[0]
    height, width = x_ref.shape
    depth = height // BAND
    chunks, team, _, lane = p_in.shape
    part = chunks * lane
    half = sweeps // 2
    group, member = d // team, d % team
    groups = nrows // team
    place = v_all.at[pl.ds(pl.multiple_of(c * own, own), own)]
    mine = pltpu.make_async_copy(v_hbm, place, v_local)
    mine.start()
    begins = pltpu.make_async_copy(starts_hbm, starts_ref, s_sem)
    begins.start()
    load = pltpu.make_async_copy(x_hbm, x_ref, x_sem)

    offsets = (-2, -1, 1, 2)

    def there(offset):
        return group + offset >= 0 if offset < 0 else group + offset < groups

    def mate(step):
        return (member + step) % team

    last = ncols - 1
    base = group * team
    barrier = pltpu.get_barrier_semaphore()

    def greet(sem, slab, core):
        pl.semaphore_signal(sem, inc=1, device_id=(slab, core), device_id_type=MESH)

    @pl.when(c > 0)
    def _():
        greet(barrier, d, 0)

    @pl.when((member < team - 1) | (c < last))
    def _():
        greet(barrier, base + team - 1, last)
    for offset in offsets:
        @pl.when(there(offset))
        def _():
            greet(barrier, base + offset * team, last)
    z_all[0] = jnp.zeros_like(z_all[0])
    z_all[team] = jnp.zeros_like(z_all[0])
    for i, offset in enumerate(offsets):
        @pl.when(jnp.logical_not(there(offset)))
        def _():
            ltp_in[i] = jnp.zeros_like(ltp_in[i])
            if abs(offset) == 1:
                near_in[:, i - 1] = jnp.zeros_like(near_in[:, 0])
            else:
                far_in[:, i // 3] = jnp.zeros_like(far_in[:, 0])
    load.start()

    @pl.when(c == 0)
    def _():
        pl.semaphore_wait(barrier, last)
        for core in range(1, ncols):
            greet(paired, d, core)

    @pl.when(c > 0)
    def _():
        pl.semaphore_wait(paired, 1)

    mine.wait()
    copies = []
    for step in range(1, ncols):
        copy = pltpu.make_async_remote_copy(
            src_ref=place, dst_ref=place, send_sem=v_send.at[step - 1], recv_sem=v_recv.at[step - 1],
            device_id=(d, (c + step) % ncols), device_id_type=MESH)
        copy.start()
        copies.append(copy)

    @pl.when((member == team - 1) & (c == last))
    def _():
        pl.semaphore_wait(barrier, ncols * team - 1)
        for slab in range(team):
            for core in range(ncols):
                if slab < team - 1 or core < last:
                    greet(entered, base + slab, core)

    begins.wait()
    across = jnp.broadcast_to(starts_ref[...], (sweeps, sweeps))
    begin = jnp.sum(jnp.where(on_diagonal(across.shape), across, 0), axis=1, keepdims=True)
    row = lax.broadcasted_iota(jnp.int32, v_all.shape, 1)
    window = (row - begin + BAND) // BAND
    outside = ((window == 0) & (d == 0)) | ((window == depth) & (d == nrows - 1) & (begin > 0))
    load.wait()
    x_halves = halves(x_ref[...])
    for copy in copies:
        copy.wait_recv()

    v = v_all[...]
    v = jnp.where(outside, 0.0, v)
    parts = [jnp.where(window == k, v, 0.0) for k in range(depth + 1)]
    u_s = jnp.concatenate([parts[0], parts[depth]], axis=0)
    u_i = jnp.concatenate(parts[1:depth], axis=0)
    inside = u_i.shape[0]
    edge = 2 * sweeps
    half_s = 0.5 * jnp.sum(u_s * u_s, axis=1, keepdims=True)
    half_i = 0.5 * jnp.sum(u_i * u_i, axis=1, keepdims=True)
    half_i = jnp.concatenate([half_i, jnp.zeros((LANES - inside, 1), jnp.float32)], axis=0)
    pad = jnp.zeros((LANES - edge, height), jnp.float32)
    us_h, ui_h = halves(u_s), halves(u_i)
    all_h = halves(jnp.concatenate(
        [u_i, jnp.zeros((LANES - inside, height), jnp.float32), u_s, pad], axis=0))
    g = gram(tuple(a[:LANES + edge] for a in all_h), all_h)
    g_ii, n_is = g[:LANES, :LANES], lower(g[:LANES, LANES:], sweeps)
    n_si, g_ss = lower(g[LANES:, :LANES], sweeps), g[LANES:, LANES:]
    l_ii = jnp.where(on_diagonal(g_ii.shape), half_i, lower(g_ii, sweeps))
    n_ss = jnp.where(on_diagonal(g_ss.shape), half_s, lower(g_ss, sweeps))
    wi_h = halves(product(ui_h, x_halves))
    w_s = product(us_h, x_halves)
    t, f = inverse(l_ii, sweeps, 2, seed_pairs(l_ii, sweeps), halves(n_is))
    nsi_h = halves(n_si)
    lt_in[member] = packed(n_ss - exact(nsi_h, halves(f)), sweeps)
    t_h = halves(t)
    k_h = tuple(a[:, :inside] for a in halves(exact(nsi_h, t_h)))
    t_h = tuple(a[:inside, :inside] for a in t_h)

    def to_mate(step, src, dst, send, recv):
        return pltpu.make_async_remote_copy(
            src_ref=src, dst_ref=dst, send_sem=send, recv_sem=recv,
            device_id=(base + mate(step), c), device_id_type=MESH)

    def lt_copy(step, core):
        return pltpu.make_async_remote_copy(
            src_ref=lt_in.at[member], dst_ref=lt_in.at[member], send_sem=l_send.at[step - 1, core],
            recv_sem=l_recv.at[step - 1], device_id=(base + mate(step), core), device_id_type=MESH)

    def p_copy(step, ch):
        return to_mate(step, p_out.at[ch, mate(step)], p_in.at[ch, member],
                       p_send.at[step - 1, ch], p_recv.at[step - 1, ch])

    def z_copy(step):
        return to_mate(step, z_all.at[pl.ds(mate(step), 2)], z_in.at[member],
                       z_send.at[step - 1], z_recv.at[step - 1])

    def y_copy(step, ch):
        return to_mate(step, y_in.at[ch, member], y_in.at[ch, member],
                       y_send.at[step - 1, ch], y_recv.at[step - 1, ch])

    def b_copy(i, slot, core):
        return pltpu.make_async_remote_copy(
            src_ref=ltp_ref.at[i // 2], dst_ref=ltp_in.at[slot], send_sem=b_send.at[i, core],
            recv_sem=b_recv.at[slot], device_id=(d + offsets[i] * team, core), device_id_type=MESH)

    def q_copy(i, slot, ch):
        if offsets[i] == -2:
            src, dst = q_ref.at[ch, 0], far_in.at[ch, 1]
        elif offsets[i] == -1:
            src, dst = q_ref.at[ch, pl.ds(0, 3)], near_in.at[ch, 1]
        elif offsets[i] == 1:
            src, dst = q_ref.at[ch, pl.ds(2, 3)], near_in.at[ch, 0]
        else:
            src, dst = q_ref.at[ch, 2], far_in.at[ch, 0]
        return pltpu.make_async_remote_copy(
            src_ref=src, dst_ref=dst, send_sem=q_send.at[i, ch], recv_sem=q_recv.at[slot, ch],
            device_id=(d + offsets[i] * team, c), device_id_type=MESH)

    @pl.when((member < team - 1) | (c < last))
    def _():
        pl.semaphore_wait(entered, 1)

    @pl.when(c == last)
    def _():
        for core in range(ncols):
            for step in range(1, team):
                lt_copy(step, core).start()

    for ch in range(chunks):
        cols = slice(ch * team * lane, (ch + 1) * team * lane)
        p = w_s[:, cols] - product(k_h, tuple(a[:, cols] for a in wi_h))
        for j in range(team):
            p_out[ch, j] = p[:, j * lane:(j + 1) * lane]
        for step in range(1, team):
            p_copy(step, ch).start()
        p_in[ch, member] = p_out[ch, member]

    peers = sum(there(offset).astype(jnp.int32) for offset in offsets)

    @pl.when((member == 0) & (c == last))
    def _():
        pl.semaphore_wait(barrier, peers * ncols * team)
        for slab in range(team):
            for core in range(ncols):
                if slab > 0 or core < last:
                    greet(arrived, base + slab, core)

    u_t = u_i.T
    ut_h = halves(u_t)
    inner = product(t_h, wi_h)
    ax_ref[...] = x_ref[...] - product(ut_h, halves(inner))
    cm_h = halves(u_s.T - product(ut_h, halves(f[:inside, :edge])))

    for step in range(1, team):
        lt_copy(step, 0).wait_recv()
    zero = jnp.zeros((sweeps, LANES), jnp.float32)
    blocks = [zero] * (team + 1)
    for j in range(team):
        for side, rows in enumerate(unpacked(lt_in[j], sweeps, j * sweeps)):
            blocks[j + side] = blocks[j + side] + rows
    first = lanes_of(blocks[0]) < sweeps
    keep = [jnp.where(first, 0.0, block) for block in blocks]
    ends = [jnp.where(first, block, 0.0) for block in blocks]
    m_ii = jnp.concatenate([zero] + keep[1:team], axis=0)
    m_si = jnp.concatenate([keep[0], keep[team]], axis=0)
    left = [zero] * team
    left[1] = left[1] + ends[1]
    left[team - 1] = left[team - 1] + pltpu.roll(ends[team - 1], sweeps, 1)
    m_is = jnp.concatenate(left, axis=0)
    m_ss = jnp.concatenate([ends[0], pltpu.roll(ends[team], sweeps, 1)], axis=0)
    tt, ff = inverse(m_ii, sweeps, depth, seed(m_ii, depth), halves(m_is))
    msi_h = halves(m_si)
    ltp = m_ss - exact(msi_h, halves(ff))
    at_l, at_r = ltp[:sweeps], ltp[sweeps:]
    early = lax.broadcasted_iota(jnp.int32, zero.shape, 0) < half
    beside = (lanes_of(zero) >= sweeps) & (lanes_of(zero) < sweeps + half)
    to_left = jnp.where(first, at_l, jnp.where(beside, jnp.where(early, at_r, at_l), 0.0))
    to_right = jnp.where(first, turn(at_r, -sweeps), jnp.where(
        beside, turn(jnp.where(early, at_l, at_r), sweeps), 0.0))
    for side, rows in enumerate((to_left, to_right)):
        ltp_ref[side] = rows[:half] + turn(rows[half:], edge)
    @pl.when((member > 0) | (c < last))
    def _():
        pl.semaphore_wait(arrived, 1)

    for i, offset in enumerate(offsets):
        @pl.when(there(offset) & (c == last))
        def _():
            for core in range(ncols):
                b_copy(i, 3 - i, core).start()
    tt_h = halves(tt)
    kk_h = halves(exact(msi_h, tt_h))
    sums = []
    for ch in range(chunks):
        for step in range(1, team):
            p_copy(step, ch).wait_recv()
        rows = [jnp.zeros((sweeps, lane), jnp.float32)]
        for j in range(1, team):
            rows.append(p_in[ch, j - 1, sweeps:] + p_in[ch, j, :sweeps])
        q_i = halves(jnp.concatenate(rows, axis=0))
        q_s = jnp.concatenate([p_in[ch, 0, :sweeps], p_in[ch, team - 1, sweeps:]], axis=0)
        q = q_s - product(kk_h, q_i)
        for j in range(4):
            q_ref[ch, j] = q[j * half:(j + 1) * half]
        q_ref[ch, 4] = q[:half]
        for i, offset in enumerate(offsets):
            @pl.when(there(offset))
            def _():
                q_copy(i, 3 - i, ch).start()
        sums.append(q_i)
    z_i = product(tt_h, tuple(jnp.concatenate(halfs, axis=1) for halfs in zip(*sums)))
    for j in range(1, team):
        z_all[j] = z_i[j * sweeps:(j + 1) * sweeps]
    for step in range(1, team):
        z_copy(step).start()
    at_left = jnp.where(on_diagonal(zero.shape), 1.0, 0.0)
    follow[0] = at_left
    for j in range(1, team):
        follow[j] = -ff[j * sweeps:(j + 1) * sweeps]
    follow[team] = turn(at_left, sweeps)
    mine_h = halves(follow[pl.ds(member, 2)].reshape(edge, LANES))
    cf_h = halves(product(cm_h, mine_h)[:, :edge])
    cf3 = jnp.concatenate([cf_h[0], cf_h[1], cf_h[0]], axis=1)

    for i, offset in enumerate(offsets):
        @pl.when(there(offset))
        def _():
            b_copy(i, i, 0).wait_recv()
    def at(rows, low, high):
        return jnp.where((lanes_of(rows) >= low) & (lanes_of(rows) < high), rows, 0.0)

    far_l, near_l, near_r, far_r = (ltp_in[i] for i in range(4))
    up, down = turn(near_l, sweeps), turn(near_l, -sweeps)
    late = jnp.zeros((half, LANES), jnp.float32)
    big = jnp.concatenate([
        at(far_l + down, 0, half),
        late,
        at(up, sweeps, 2 * sweeps),
        at(down, sweeps, 2 * sweeps) + at(up, 0, half),
        at(turn(near_r, 2 * sweeps), 2 * sweeps, 3 * sweeps),
        at(near_r, 2 * sweeps, 3 * sweeps + half),
        at(turn(near_r, 2 * sweeps) + turn(far_r, 3 * sweeps), 3 * sweeps, 3 * sweeps + half),
        late,
    ], axis=0)
    here = turn(ltp, sweeps)
    big = big + jnp.concatenate([zero, here, zero], axis=0)
    s_h = halves(inverse(big, sweeps, half // 2, seed(big, half // 2))[sweeps:3 * sweeps])

    none = jnp.zeros((half, lane), jnp.float32)
    for ch in range(chunks):
        for i, offset in enumerate(offsets):
            @pl.when(there(offset))
            def _():
                q_copy(i, i, ch).wait_recv()
        rhs = jnp.concatenate([
            far_in[ch, 0] + near_in[ch, 0, 2],
            none,
            near_in[ch, 0, 0] + q_ref[ch, 0],
            near_in[ch, 0, 1] + q_ref[ch, 1],
            q_ref[ch, 2] + near_in[ch, 1, 0],
            q_ref[ch, 3] + near_in[ch, 1, 1],
            near_in[ch, 1, 2] + far_in[ch, 1],
            none,
        ], axis=0)
        y_in[ch, member] = product(s_h, halves(rhs))
        for step in range(1, team):
            y_copy(step, ch).start()

    cm3 = jnp.concatenate([cm_h[0], cm_h[1], cm_h[0]], axis=1)

    def apply(left, y):
        y_h = halves(y)
        y3 = jnp.concatenate([y_h[0], y_h[0], y_h[1]], axis=0)
        return lax.dot_general(left, y3, (((1,), (0,)), ((), ())), preferred_element_type=jnp.float32)

    z_in[member] = z_all[pl.ds(member, 2)]
    for step in range(1, team):
        z_copy(step).wait_recv()
    span = team * lane
    for ch in range(chunks):
        z = jnp.concatenate(
            [z_in[j].reshape(edge, part)[:, ch * lane:(ch + 1) * lane] for j in range(team)], axis=1)
        cols = slice(ch * span, (ch + 1) * span)
        ax_ref[:, cols] = ax_ref[:, cols] - apply(cm3, z)

    for ch in range(chunks - 1):
        for step in range(1, team):
            y_copy(step, ch).wait_recv()
        cols = slice(ch * span, (ch + 1) * span)
        y = jnp.concatenate([y_in[ch, j] for j in range(team)], axis=1)
        out_ref[:, cols] = ax_ref[:, cols] - apply(cf3, y)

    def last_step(j):
        cols = pl.ds(pl.multiple_of(((chunks - 1) * team + j) * lane, lane), lane)
        out_ref[:, cols] = ax_ref[:, cols] - apply(cf3, y_in[chunks - 1, j])

    last_step(member)
    for step in range(1, team):
        y_copy(step, chunks - 1).wait_recv()
        last_step(mate(team - step))

    for copy in copies:
        copy.wait_send()
    for step in range(1, team):
        for ch in range(chunks):
            p_copy(step, ch).wait_send()
            y_copy(step, ch).wait_send()
        z_copy(step).wait_send()
    for i, offset in enumerate(offsets):
        @pl.when(there(offset))
        def _():
            for ch in range(chunks):
                q_copy(i, 3 - i, ch).wait_send()

    @pl.when(c == last)
    def _():
        for core in range(ncols):
            for step in range(1, team):
                lt_copy(step, core).wait_send()
            for i, offset in enumerate(offsets):
                @pl.when(there(offset))
                def _():
                    b_copy(i, 3 - i, core).wait_send()


def per_device(nrows, ncols, eigvecs, reflectors, starts):
    height, width = eigvecs.shape
    sweeps = starts.shape[0]
    team = sweeps // (2 * (height // BAND))
    part = width // team
    lane = LANES
    chunks = part // lane
    assert team * sweeps == LANES and nrows % team == 0
    f32 = jnp.float32
    hbm = pl.BlockSpec(memory_space=pltpu.HBM)
    dma = pltpu.SemaphoreType.DMA
    return pl.pallas_call(
        functools.partial(kernel, nrows, ncols),
        out_shape=jax.ShapeDtypeStruct((height, width), f32),
        in_specs=[hbm, hbm, hbm],
        out_specs=pl.BlockSpec(memory_space=pltpu.VMEM),
        scratch_shapes=[
            pltpu.VMEM((height, width), f32),
            pltpu.VMEM((sweeps, height), f32),
            pltpu.VMEM((1, sweeps), jnp.int32),
            pltpu.VMEM((team, sweeps, LANES), f32),
            pltpu.VMEM((chunks, team, 2 * sweeps, lane), f32),
            pltpu.VMEM((chunks, team, 2 * sweeps, lane), f32),
            pltpu.VMEM((2, sweeps // 2, LANES), f32),
            pltpu.VMEM((4, sweeps // 2, LANES), f32),
            pltpu.VMEM((team + 1, sweeps, LANES), f32),
            pltpu.VMEM((chunks, 5, sweeps // 2, lane), f32),
            pltpu.VMEM((chunks, 2, 3, sweeps // 2, lane), f32),
            pltpu.VMEM((chunks, 2, sweeps // 2, lane), f32),
            pltpu.VMEM((team + 1, sweeps, part), f32),
            pltpu.VMEM((team, 2, sweeps, part), f32),
            pltpu.VMEM((chunks, team, 2 * sweeps, lane), f32),
            pltpu.VMEM((height, width), f32),
            dma, dma, dma,
            dma((ncols - 1,)), dma((ncols - 1,)),
            dma((team - 1, ncols)), dma((team - 1,)),
            dma((team - 1, chunks)), dma((team - 1, chunks)),
            dma((4, ncols)), dma((4,)),
            dma((4, chunks)), dma((4, chunks)),
            dma((team - 1,)), dma((team - 1,)),
            dma((team - 1, chunks)), dma((team - 1, chunks)),
            pltpu.SemaphoreType.REGULAR, pltpu.SemaphoreType.REGULAR, pltpu.SemaphoreType.REGULAR,
        ],
        compiler_params=pltpu.CompilerParams(
            collective_id=0, has_side_effects=True, vmem_limit_bytes=32 * 1024 * 1024),
    )(*(pltpu.with_memory_space_constraint(a, pltpu.HBM)
        for a in (eigvecs, reflectors, starts.reshape(1, sweeps))))


def solution(mesh):
    in_specs = (P("rows", "cols"), P("cols", "rows"), P())
    out_specs = P("rows", "cols")
    body = functools.partial(per_device, mesh.shape["rows"], mesh.shape["cols"])
    return jax.shard_map(
        body, mesh=mesh, in_specs=in_specs, out_specs=out_specs, check_vma=False
    )
```

time: 23.5 us -> 21.7 us (0.923)
  Pallas kernels: 22.4 us -> 20.5 us
    pallas_call x1, Pallas kernels: 22.4 us -> 20.5 us  [per_device(): pl.pallas_call(functools.partial(kernel, nrows, ncols), out_shape=jax.Sha...]
where the time goes in v4:
time: 21.7 us; the launch traced here: 21.5 us
  Pallas kernels  20.5 us (94%)
  local copies, waits for them, and re-layouts  0.97 us (4%)
    pallas_call x1, Pallas kernels, per_device(): pl.pallas_call(functools.partial(kernel, nrows, ncols), out_shape=jax.Sha...  20.5 us
    unnamed x1, local copies, waits for them, and re-layouts  0.97 us

profile of v4, /device:TPU:0, one launch (start us, length us, event | category | flops | bytes accessed | tf_op | source)
XLA Modules:
  0.0 21.5 jit_solution(17315469476214278541)
XLA Ops:
  0.0 20.5 %shard_map.37 = f32[256,1024]{1,0:T(8,128)S(1)} custom-call(f32[256,1024]{1,0:T(8,128)} %x_hbm.1, f32[16,256]{1,0:T(8,128)} %v_hbm.1, s32[1,32]{1,0:T(1,128)} %bitcast.1), custom_call_target="tpu_custom_call" | custom-call | tf_op jit(solution)/shard_map/pallas_call | solution.py:515
  20.5 1.0 %copy.5 = f32[256,1024]{1,0:T(8,128)} copy(f32[256,1024]{1,0:T(8,128)S(1)} %shard_map.37) | data formatting | bytes 2097152

commit v5 on v4

--- a/solution.py
+++ b/solution.py
@@ -176,8 +176,8 @@
         @pl.when(there(offset))
         def _():
             greet(barrier, base + offset * team, last)
-    z_all[0] = jnp.zeros_like(z_all[0])
-    z_all[team] = jnp.zeros_like(z_all[0])
+    z_all[:, 0] = jnp.zeros_like(z_all[:, 0])
+    z_all[:, team] = jnp.zeros_like(z_all[:, 0])
     for i, offset in enumerate(offsets):
         @pl.when(jnp.logical_not(there(offset)))
         def _():
@@ -221,8 +221,6 @@
     row = lax.broadcasted_iota(jnp.int32, v_all.shape, 1)
     window = (row - begin + BAND) // BAND
     outside = ((window == 0) & (d == 0)) | ((window == depth) & (d == nrows - 1) & (begin > 0))
-    load.wait()
-    x_halves = halves(x_ref[...])
     for copy in copies:
         copy.wait_recv()
 
@@ -245,8 +243,6 @@
     n_si, g_ss = lower(g[LANES:, :LANES], sweeps), g[LANES:, LANES:]
     l_ii = jnp.where(on_diagonal(g_ii.shape), half_i, lower(g_ii, sweeps))
     n_ss = jnp.where(on_diagonal(g_ss.shape), half_s, lower(g_ss, sweeps))
-    wi_h = halves(product(ui_h, x_halves))
-    w_s = product(us_h, x_halves)
     t, f = inverse(l_ii, sweeps, 2, seed_pairs(l_ii, sweeps), halves(n_is))
     nsi_h = halves(n_si)
     lt_in[member] = packed(n_ss - exact(nsi_h, halves(f)), sweeps)
@@ -268,12 +264,18 @@
         return to_mate(step, p_out.at[ch, mate(step)], p_in.at[ch, member],
                        p_send.at[step - 1, ch], p_recv.at[step - 1, ch])
 
-    def z_copy(step):
-        return to_mate(step, z_all.at[pl.ds(mate(step), 2)], z_in.at[member],
-                       z_send.at[step - 1], z_recv.at[step - 1])
+    def z_copy(step, ch):
+        return to_mate(step, z_all.at[ch, pl.ds(mate(step), 2)], z_in.at[ch, member],
+                       z_send.at[step - 1, ch], z_recv.at[step - 1, ch])
+
+    read = -(-(edge - depth * (team - 1)) // 8) * 8
+
+    def reads(j):
+        return depth * j // 8 * 8
 
     def y_copy(step, ch):
-        return to_mate(step, y_in.at[ch, member], y_in.at[ch, member],
+        rows = pl.ds(pl.multiple_of(reads(mate(step)), 8), read)
+        return to_mate(step, y_in.at[ch, member, rows], y_in.at[ch, member, rows],
                        y_send.at[step - 1, ch], y_recv.at[step - 1, ch])
 
     def b_copy(i, slot, core):
@@ -304,9 +306,14 @@
             for step in range(1, team):
                 lt_copy(step, core).start()
 
+    load.wait()
+    span = team * lane
+    slices = [slice(ch * span, (ch + 1) * span) for ch in range(chunks)]
+    wi_h = []
     for ch in range(chunks):
-        cols = slice(ch * team * lane, (ch + 1) * team * lane)
-        p = w_s[:, cols] - product(k_h, tuple(a[:, cols] for a in wi_h))
+        x_h = halves(x_ref[:, slices[ch]])
+        wi_h.append(halves(product(ui_h, x_h)))
+        p = product(us_h, x_h) - product(k_h, wi_h[ch])
         for j in range(team):
             p_out[ch, j] = p[:, j * lane:(j + 1) * lane]
         for step in range(1, team):
@@ -325,8 +332,9 @@
 
     u_t = u_i.T
     ut_h = halves(u_t)
-    inner = product(t_h, wi_h)
-    ax_ref[...] = x_ref[...] - product(ut_h, halves(inner))
+    for ch, cols in enumerate(slices):
+        inner = product(t_h, wi_h[ch])
+        ax_ref[:, cols] = x_ref[:, cols] - product(ut_h, halves(inner))
     cm_h = halves(u_s.T - product(ut_h, halves(f[:inside, :edge])))
 
     for step in range(1, team):
@@ -368,7 +376,6 @@
                 b_copy(i, 3 - i, core).start()
     tt_h = halves(tt)
     kk_h = halves(exact(msi_h, tt_h))
-    sums = []
     for ch in range(chunks):
         for step in range(1, team):
             p_copy(step, ch).wait_recv()
@@ -385,17 +392,20 @@
             @pl.when(there(offset))
             def _():
                 q_copy(i, 3 - i, ch).start()
-        sums.append(q_i)
-    z_i = product(tt_h, tuple(jnp.concatenate(halfs, axis=1) for halfs in zip(*sums)))
-    for j in range(1, team):
-        z_all[j] = z_i[j * sweeps:(j + 1) * sweeps]
-    for step in range(1, team):
-        z_copy(step).start()
-    at_left = jnp.where(on_diagonal(zero.shape), 1.0, 0.0)
-    follow[0] = at_left
+        z_i = product(tt_h, q_i)
+        for j in range(1, team):
+            z_all[ch, j] = z_i[j * sweeps:(j + 1) * sweeps]
+        for step in range(1, team):
+            z_copy(step, ch).start()
+    new = lanes_of(m_ii)
+    new = jnp.where(new < sweeps, sweeps - 8 - new + 2 * (new % 8), new)
+    order = (lax.broadcasted_iota(jnp.int32, new.shape, 0) == new).astype(jnp.bfloat16)
+    ff = sum(lax.dot_general(a, order, (((1,), (0,)), ((), ())), preferred_element_type=jnp.float32)
+             for a in halves(ff))
+    follow[0] = order[:sweeps].astype(jnp.float32)
     for j in range(1, team):
         follow[j] = -ff[j * sweeps:(j + 1) * sweeps]
-    follow[team] = turn(at_left, sweeps)
+    follow[team] = order[sweeps:edge].astype(jnp.float32)
     mine_h = halves(follow[pl.ds(member, 2)].reshape(edge, LANES))
     cf_h = halves(product(cm_h, mine_h)[:, :edge])
     cf3 = jnp.concatenate([cf_h[0], cf_h[1], cf_h[0]], axis=1)
@@ -422,7 +432,9 @@
     ], axis=0)
     here = turn(ltp, sweeps)
     big = big + jnp.concatenate([zero, here, zero], axis=0)
-    s_h = halves(inverse(big, sweeps, half // 2, seed(big, half // 2))[sweeps:3 * sweeps])
+    full = inverse(big, sweeps, half // 2, seed(big, half // 2))[sweeps:3 * sweeps]
+    s_h = halves(jnp.concatenate(
+        [full[b:b + 8] for b in range(sweeps - 8, -1, -8)] + [full[sweeps:]], axis=0))
 
     none = jnp.zeros((half, lane), jnp.float32)
     for ch in range(chunks):
@@ -451,26 +463,27 @@
         y3 = jnp.concatenate([y_h[0], y_h[0], y_h[1]], axis=0)
         return lax.dot_general(left, y3, (((1,), (0,)), ((), ())), preferred_element_type=jnp.float32)
 
-    z_in[member] = z_all[pl.ds(member, 2)]
-    for step in range(1, team):
-        z_copy(step).wait_recv()
-    span = team * lane
     for ch in range(chunks):
-        z = jnp.concatenate(
-            [z_in[j].reshape(edge, part)[:, ch * lane:(ch + 1) * lane] for j in range(team)], axis=1)
-        cols = slice(ch * span, (ch + 1) * span)
+        z_in[ch, member] = z_all[ch, pl.ds(member, 2)]
+    for ch, cols in enumerate(slices):
+        for step in range(1, team):
+            z_copy(step, ch).wait_recv()
+        z = jnp.concatenate([z_in[ch, j].reshape(edge, lane) for j in range(team)], axis=1)
         ax_ref[:, cols] = ax_ref[:, cols] - apply(cm3, z)
+
+    row = lax.broadcasted_iota(jnp.int32, (edge, lane), 0)
+    sent = (row >= reads(member)) & (row < reads(member) + read)
 
     for ch in range(chunks - 1):
         for step in range(1, team):
             y_copy(step, ch).wait_recv()
-        cols = slice(ch * span, (ch + 1) * span)
-        y = jnp.concatenate([y_in[ch, j] for j in range(team)], axis=1)
+        cols = slices[ch]
+        y = jnp.concatenate([jnp.where(sent, y_in[ch, j], 0.0) for j in range(team)], axis=1)
         out_ref[:, cols] = ax_ref[:, cols] - apply(cf3, y)
 
     def last_step(j):
         cols = pl.ds(pl.multiple_of(((chunks - 1) * team + j) * lane, lane), lane)
-        out_ref[:, cols] = ax_ref[:, cols] - apply(cf3, y_in[chunks - 1, j])
+        out_ref[:, cols] = ax_ref[:, cols] - apply(cf3, jnp.where(sent, y_in[chunks - 1, j], 0.0))
 
     last_step(member)
     for step in range(1, team):
@@ -482,8 +495,8 @@
     for step in range(1, team):
         for ch in range(chunks):
             p_copy(step, ch).wait_send()
+            z_copy(step, ch).wait_send()
             y_copy(step, ch).wait_send()
-        z_copy(step).wait_send()
     for i, offset in enumerate(offsets):
         @pl.when(there(offset))
         def _():
@@ -530,8 +543,8 @@
             pltpu.VMEM((chunks, 5, sweeps // 2, lane), f32),
             pltpu.VMEM((chunks, 2, 3, sweeps // 2, lane), f32),
             pltpu.VMEM((chunks, 2, sweeps // 2, lane), f32),
-            pltpu.VMEM((team + 1, sweeps, part), f32),
-            pltpu.VMEM((team, 2, sweeps, part), f32),
+            pltpu.VMEM((chunks, team + 1, sweeps, lane), f32),
+            pltpu.VMEM((chunks, team, 2, sweeps, lane), f32),
             pltpu.VMEM((chunks, team, 2 * sweeps, lane), f32),
             pltpu.VMEM((height, width), f32),
             dma, dma, dma,
@@ -540,7 +553,7 @@
             dma((team - 1, chunks)), dma((team - 1, chunks)),
             dma((4, ncols)), dma((4,)),
             dma((4, chunks)), dma((4, chunks)),
-            dma((team - 1,)), dma((team - 1,)),
+            dma((team - 1, chunks)), dma((team - 1, chunks)),
             dma((team - 1, chunks)), dma((team - 1, chunks)),
             pltpu.SemaphoreType.REGULAR, pltpu.SemaphoreType.REGULAR, pltpu.SemaphoreType.REGULAR,
         ],

time: 21.7 us -> 21.3 us (0.982)
  Pallas kernels: 20.5 us -> 20.2 us
    pallas_call x1, Pallas kernels: 20.5 us -> 20.2 us  [per_device(): pl.pallas_call(functools.partial(kernel, nrows, ncols), out_shape=jax.Sha...]
where the time goes in v5:
time: 21.3 us; the launch traced here: 21.1 us
  Pallas kernels  20.2 us (95%)
  local copies, waits for them, and re-layouts  0.97 us (5%)
    pallas_call x1, Pallas kernels, per_device(): pl.pallas_call(functools.partial(kernel, nrows, ncols), out_shape=jax.Sha...  20.2 us
    unnamed x1, local copies, waits for them, and re-layouts  0.97 us

profile of v5, /device:TPU:0, one launch (start us, length us, event | category | flops | bytes accessed | tf_op | source)
XLA Modules:
  0.0 21.1 jit_solution(14709726672098650467)
XLA Ops:
  0.0 20.2 %shard_map.37 = f32[256,1024]{1,0:T(8,128)S(1)} custom-call(f32[256,1024]{1,0:T(8,128)} %x_hbm.1, f32[16,256]{1,0:T(8,128)} %v_hbm.1, s32[1,32]{1,0:T(1,128)} %bitcast.1), custom_call_target="tpu_custom_call" | custom-call | tf_op jit(solution)/shard_map/pallas_call | solution.py:528
  20.2 1.0 %copy.5 = f32[256,1024]{1,0:T(8,128)} copy(f32[256,1024]{1,0:T(8,128)S(1)} %shard_map.37) | data formatting | bytes 2097152

commit v6 on v5

--- a/solution.py
+++ b/solution.py
@@ -72,36 +72,30 @@
 
 def seed(full, size):
     lanes = full.shape[1]
-    eye = on_diagonal(full.shape)
-    diag = jnp.where(eye, full, 0.0)
-    down = jnp.sum(diag, axis=1, keepdims=True)
-    across = jnp.sum(diag, axis=0, keepdims=True)
-    down = 1.0 / jnp.where(down == 0.0, 1.0, down)
-    across = 1.0 / jnp.where(across == 0.0, 1.0, across)
     rows = lax.broadcasted_iota(jnp.int32, full.shape, 0)
     cols = lax.broadcasted_iota(jnp.int32, full.shape, 1)
-    scaled = jnp.where((rows ^ cols) < size, down * full, 0.0)
-    below = [jnp.where(rows - cols == m, scaled, 0.0) for m in range(size)]
-    below = [jnp.sum(entries, axis=0, keepdims=True) for entries in below]
+    own = jnp.where((rows ^ cols) < size, full, 0.0)
+    below = [jnp.sum(jnp.where(rows - cols == m, own, 0.0), axis=0, keepdims=True)
+             for m in range(size)]
+    across = 1.0 / jnp.where(below[0] == 0.0, 1.0, below[0])
+
+    def ahead(a, by):
+        return pltpu.roll(a, lanes - by, 1) if by else a
+
     terms = [across]
     for k in range(1, size):
-        total = below[k] * across
-        for m in range(1, k):
-            total = total + pltpu.roll(below[m], lanes - (k - m), 1) * terms[k - m]
-        terms.append(-total)
-    done = jnp.where(eye, across, 0.0)
+        total = sum(ahead(below[m], k - m) * terms[k - m] for m in range(1, k + 1))
+        terms.append(-ahead(across, k) * total)
+    done = jnp.where(rows == cols, across, 0.0)
     for k in range(1, size):
         done = jnp.where(rows - cols == k, terms[k], done)
     return done
 
 
-def seed_pairs(full, sweeps):
+def seed_pairs(full, sweeps, diag):
     eye = on_diagonal(full.shape)
-    diag = jnp.where(eye, full, 0.0)
-    down = jnp.sum(diag, axis=1, keepdims=True)
-    across = jnp.sum(diag, axis=0, keepdims=True)
-    down = 1.0 / jnp.where(down == 0.0, 1.0, down)
-    across = 1.0 / jnp.where(across == 0.0, 1.0, across)
+    down = 1.0 / jnp.where(diag == 0.0, 1.0, diag)
+    across = jnp.sum(jnp.where(eye, down, 0.0), axis=0, keepdims=True)
     rows, cols = sweep_pair(full.shape, sweeps)
     pair = ((rows ^ cols) == 1) & (rows > cols)
     return jnp.where(eye, down, 0.0) - down * jnp.where(pair, full, 0.0) * across
@@ -243,7 +237,7 @@
     n_si, g_ss = lower(g[LANES:, :LANES], sweeps), g[LANES:, LANES:]
     l_ii = jnp.where(on_diagonal(g_ii.shape), half_i, lower(g_ii, sweeps))
     n_ss = jnp.where(on_diagonal(g_ss.shape), half_s, lower(g_ss, sweeps))
-    t, f = inverse(l_ii, sweeps, 2, seed_pairs(l_ii, sweeps), halves(n_is))
+    t, f = inverse(l_ii, sweeps, 2, seed_pairs(l_ii, sweeps, half_i), halves(n_is))
     nsi_h = halves(n_si)
     lt_in[member] = packed(n_ss - exact(nsi_h, halves(f)), sweeps)
     t_h = halves(t)
@@ -432,9 +426,17 @@
     ], axis=0)
     here = turn(ltp, sweeps)
     big = big + jnp.concatenate([zero, here, zero], axis=0)
-    full = inverse(big, sweeps, half // 2, seed(big, half // 2))[sweeps:3 * sweeps]
-    s_h = halves(jnp.concatenate(
-        [full[b:b + 8] for b in range(sweeps - 8, -1, -8)] + [full[sweeps:]], axis=0))
+    def own_rows(a):
+        blocks = [a[b:b + 8] for b in range(2 * sweeps - 8, sweeps - 1, -8)]
+        return jnp.concatenate(blocks + [a[2 * sweeps:3 * sweeps]], axis=0)
+
+    apart = [axis & (sweeps - 1) for axis in (
+        lax.broadcasted_iota(jnp.int32, big.shape, 0), lax.broadcasted_iota(jnp.int32, big.shape, 1))]
+    off = jnp.where((apart[0] >= half) & (apart[1] < half), big, 0.0)
+    done = seed(big, half)
+    near = own_rows(done)
+    step = exact(halves(near), halves(off))
+    s_h = halves(near - exact(halves(step), halves(done)))
 
     none = jnp.zeros((half, lane), jnp.float32)
     for ch in range(chunks):

time: 21.3 us -> 21.2 us (level)
  no operation moved by 1% of the time
where the time goes in v6:
time: 21.2 us; the launch traced here: 21.1 us
  Pallas kernels  20.1 us (95%)
  local copies, waits for them, and re-layouts  0.97 us (5%)
    pallas_call x1, Pallas kernels, per_device(): pl.pallas_call(functools.partial(kernel, nrows, ncols), out_shape=jax.Sha...  20.1 us
    unnamed x1, local copies, waits for them, and re-layouts  0.97 us

profile of v6, /device:TPU:0, one launch (start us, length us, event | category | flops | bytes accessed | tf_op | source)
XLA Modules:
  0.0 21.1 jit_solution(11269063871841594691)
XLA Ops:
  0.0 20.1 %shard_map.37 = f32[256,1024]{1,0:T(8,128)S(1)} custom-call(f32[256,1024]{1,0:T(8,128)} %x_hbm.1, f32[16,256]{1,0:T(8,128)} %v_hbm.1, s32[1,32]{1,0:T(1,128)} %bitcast.1), custom_call_target="tpu_custom_call" | custom-call | tf_op jit(solution)/shard_map/pallas_call | solution.py:530
  20.1 1.0 %copy.5 = f32[256,1024]{1,0:T(8,128)} copy(f32[256,1024]{1,0:T(8,128)S(1)} %shard_map.37) | data formatting | bytes 2097152

commit v7 on v6

--- a/solution.py
+++ b/solution.py
@@ -145,6 +145,7 @@
     load = pltpu.make_async_copy(x_hbm, x_ref, x_sem)
 
     offsets = (-2, -1, 1, 2)
+    far_first = sorted(enumerate(offsets), key=lambda item: -abs(item[1]))
 
     def there(offset):
         return group + offset >= 0 if offset < 0 else group + offset < groups
@@ -363,7 +364,7 @@
     def _():
         pl.semaphore_wait(arrived, 1)
 
-    for i, offset in enumerate(offsets):
+    for i, offset in far_first:
         @pl.when(there(offset) & (c == last))
         def _():
             for core in range(ncols):
@@ -382,7 +383,7 @@
         for j in range(4):
             q_ref[ch, j] = q[j * half:(j + 1) * half]
         q_ref[ch, 4] = q[:half]
-        for i, offset in enumerate(offsets):
+        for i, offset in far_first:
             @pl.when(there(offset))
             def _():
                 q_copy(i, 3 - i, ch).start()

time: 21.2 us -> 21.2 us (level)
  no operation moved by 1% of the time
where the time goes in v7:
time: 21.2 us; the launch traced here: 21 us
  Pallas kernels  20.1 us (95%)
  local copies, waits for them, and re-layouts  0.97 us (5%)
    pallas_call x1, Pallas kernels, per_device(): pl.pallas_call(functools.partial(kernel, nrows, ncols), out_shape=jax.Sha...  20.1 us
    unnamed x1, local copies, waits for them, and re-layouts  0.97 us

profile of v7, /device:TPU:0, one launch (start us, length us, event | category | flops | bytes accessed | tf_op | source)
XLA Modules:
  0.0 21.0 jit_solution(13157853337316294089)
XLA Ops:
  0.0 20.1 %shard_map.37 = f32[256,1024]{1,0:T(8,128)S(1)} custom-call(f32[256,1024]{1,0:T(8,128)} %x_hbm.1, f32[16,256]{1,0:T(8,128)} %v_hbm.1, s32[1,32]{1,0:T(1,128)} %bitcast.1), custom_call_target="tpu_custom_call" | custom-call | tf_op jit(solution)/shard_map/pallas_call | solution.py:531
  20.1 1.0 %copy.5 = f32[256,1024]{1,0:T(8,128)} copy(f32[256,1024]{1,0:T(8,128)S(1)} %shard_map.37) | data formatting | bytes 2097152

commit v8 on v7

--- a/solution.py
+++ b/solution.py
@@ -145,6 +145,7 @@
     load = pltpu.make_async_copy(x_hbm, x_ref, x_sem)
 
     offsets = (-2, -1, 1, 2)
+    far_mates = sorted(range(1, team), key=lambda step: step % 2 == 0)
     far_first = sorted(enumerate(offsets), key=lambda item: -abs(item[1]))
 
     def there(offset):
@@ -311,7 +312,7 @@
         p = product(us_h, x_h) - product(k_h, wi_h[ch])
         for j in range(team):
             p_out[ch, j] = p[:, j * lane:(j + 1) * lane]
-        for step in range(1, team):
+        for step in far_mates:
             p_copy(step, ch).start()
         p_in[ch, member] = p_out[ch, member]
 
@@ -456,7 +457,7 @@
             none,
         ], axis=0)
         y_in[ch, member] = product(s_h, halves(rhs))
-        for step in range(1, team):
+        for step in far_mates:
             y_copy(step, ch).start()
 
     cm3 = jnp.concatenate([cm_h[0], cm_h[1], cm_h[0]], axis=1)

time: 21.2 us -> 21.2 us (level)
  no operation moved by 1% of the time
where the time goes in v8:
time: 21.2 us; the launch traced here: 21 us
  Pallas kernels  20.1 us (95%)
  local copies, waits for them, and re-layouts  0.97 us (5%)
    pallas_call x1, Pallas kernels, per_device(): pl.pallas_call(functools.partial(kernel, nrows, ncols), out_shape=jax.Sha...  20.1 us
    unnamed x1, local copies, waits for them, and re-layouts  0.97 us

profile of v8, /device:TPU:0, one launch (start us, length us, event | category | flops | bytes accessed | tf_op | source)
XLA Modules:
  0.0 21.0 jit_solution(4654110168433989005)
XLA Ops:
  0.0 20.1 %shard_map.37 = f32[256,1024]{1,0:T(8,128)S(1)} custom-call(f32[256,1024]{1,0:T(8,128)} %x_hbm.1, f32[16,256]{1,0:T(8,128)} %v_hbm.1, s32[1,32]{1,0:T(1,128)} %bitcast.1), custom_call_target="tpu_custom_call" | custom-call | tf_op jit(solution)/shard_map/pallas_call | solution.py:532
  20.1 1.0 %copy.5 = f32[256,1024]{1,0:T(8,128)} copy(f32[256,1024]{1,0:T(8,128)S(1)} %shard_map.37) | data formatting | bytes 2097152
